TPU v7x, 32 devices: a whole 2x2x4 slice. The times are simulated.
32 devices in a mesh: dp: 8 (over z, x), expert: 4 (over y, core).
Axes of the slice: x: 2, y: 2, z: 4, core: 2. Of those that a mesh axis runs over, the one named last changes fastest.
Arguments:
- out_grad: bfloat16 [8192, 1024], P(('dp', 'expert')), may hold values from -6 to 6
- expert_of: int32 [8192, 1], P(('dp', 'expert')), may hold values from 0 to 3; in each aligned block of 256 rows (0 to 255, 256 to 511, ...) at most 128 rows name the same one
- pre_act: bfloat16 [16384, 4096], P(('dp', 'expert')), may hold values from -6 to 6
- down_weight: bfloat16 [4, 4096, 1024], P('expert', 'dp'), may hold values from -0.09375 to 0.09375
Outputs:
- pre_grad: bfloat16 [16384, 4096], P(('dp', 'expert'))
- weight_grad: float32 [4, 4096, 1024], P('expert', 'dp')
Inputs may be any that keep to these rules, and one draw needn't show every extreme that they name: `expert_of`: within each aligned block of 256 rows (the rows of one device) no expert is named by more than 128 rows, and in some blocks one expert is named by exactly 128 rows.
All inputs are finite; a program needn't handle non-finite values.
Results may differ from a plain program's by a relative error of at most 0.0026.
Values may be sent and summed in bfloat16 or wider, within the bound.
A program may use at most 128 MiB of HBM per device.

v0:
```python
import functools
import math

import jax
import jax.numpy as jnp
from jax import lax
from jax.experimental import pallas as pl
from jax.experimental.pallas import tpu as pltpu
from jax.sharding import PartitionSpec as P

tanh_scale = 0.7978845608028654
cubic_weight = 0.044715
MESH = pl.DeviceIdType.MESH
PAIR = 2
LINE = 4
CUTS = 2


def activate(values):
    argument = tanh_scale * (values + cubic_weight * values * values * values)
    return 0.5 * values * (1.0 + jnp.tanh(argument))


def derivative(values):
    tangent = jnp.tanh(tanh_scale * (values + cubic_weight * values * values * values))
    return 0.5 * (1.0 + tangent) + 0.5 * values * (1.0 - tangent * tangent) * tanh_scale * (
        1.0 + 3.0 * cubic_weight * values * values
    )


def kernel(
    experts,
    capacity,
    factor,
    tokens_ref,
    route_ref,
    pre_hbm,
    weight_hbm,
    grad_hbm,
    dw_hbm,
    their_tokens,
    their_route,
    outgoing,
    arrived,
    pre_own,
    pre_theirs,
    weights,
    hidden,
    slope,
    partial,
    sums_out,
    sums_in,
    token_sems,
    send_sems,
    arrive_sems,
    local_sems,
    pre_sems,
    weight_send,
    weight_recv,
    sum_send,
    sum_recv,
    grad_sems,
):
    d = lax.axis_index("dp")
    me = lax.axis_index("expert")
    z = lax.div(d, PAIR)
    x = lax.rem(d, PAIR)
    partner = z * PAIR + 1 - x
    rows, width = pre_hbm.shape[0], tokens_ref.shape[1]
    block = weight_hbm.shape[0]
    count = tokens_ref.shape[0]
    low = z < LINE // 2

    def order(i):
        if i == LINE - 1:
            return z
        down = LINE - 1 - i
        return jnp.where(
            low, jnp.where(down > z, down, down - 1), jnp.where(i < z, i, i + 1)
        )

    piece = block // CUTS

    def columns(j, side):
        return pl.ds(pl.multiple_of((j * PAIR + side) * block, block), block)

    def within(cut):
        return pl.ds(pl.multiple_of(cut * piece, piece), piece)

    barrier = pltpu.get_barrier_semaphore()
    pl.semaphore_signal(barrier, inc=1, device_id={"dp": partner}, device_id_type=MESH)
    for k in range(1, experts):
        pl.semaphore_signal(
            barrier, inc=1, device_id={"expert": lax.rem(me + k, experts)}, device_id_type=MESH
        )

    @pl.when(z > 0)
    def _():
        pl.semaphore_signal(barrier, inc=1, device_id={"dp": d - PAIR}, device_id_type=MESH)

    @pl.when(z < LINE - 1)
    def _():
        pl.semaphore_signal(barrier, inc=1, device_id={"dp": d + PAIR}, device_id_type=MESH)

    inner = jnp.where((z > 0) & (z < LINE - 1), 2, 1)
    pl.semaphore_wait(barrier, experts + inner)

    def remote(src, dst, send, recv, device):
        return pltpu.make_async_remote_copy(
            src_ref=src, dst_ref=dst, send_sem=send, recv_sem=recv,
            device_id=device, device_id_type=MESH,
        )

    route_copy = remote(
        route_ref, their_route, token_sems.at[0], token_sems.at[1], {"dp": partner}
    )
    token_copy = remote(
        tokens_ref, their_tokens, token_sems.at[2], token_sems.at[3], {"dp": partner}
    )
    route_copy.start()
    token_copy.start()

    def weight_copy(direction, hop):
        step = 1 - 2 * direction
        shard = z - step * hop
        shard = jnp.clip(shard, 0, LINE - 1)
        src = weight_hbm if hop == 0 else weights.at[shard]
        return remote(
            src, weights.at[shard], weight_send.at[direction, hop],
            weight_recv.at[direction, hop], {"dp": d + step * PAIR},
        )

    def sends(direction, hop):
        if direction == 0:
            return (z >= hop) & (z < LINE - 1)
        return (z <= LINE - 1 - hop) & (z > 0)

    def receives(direction, hop):
        return (z > hop) if direction == 0 else (z < LINE - 1 - hop)

    def weight_start(hop):
        for direction in range(2):
            @pl.when(sends(direction, hop))
            def _():
                weight_copy(direction, hop).start()

    def weight_arrive(hop):
        for direction in range(2):
            @pl.when(receives(direction, hop))
            def _():
                step = 1 - 2 * direction
                shard = jnp.clip(z - step * (hop + 1), 0, LINE - 1)
                remote(
                    weight_hbm, weights.at[shard], weight_send.at[direction, hop],
                    weight_recv.at[direction, hop], {"dp": partner},
                ).wait_recv()

    weight_start(0)

    def pre_copy(i, cut):
        start = (order(i) * PAIR + 1 - x) * block + cut * piece
        return remote(
            pre_hbm.at[:, pl.ds(pl.multiple_of(start, piece), piece)],
            pre_theirs.at[i, :, within(cut)],
            pre_sems.at[0, i, cut], pre_sems.at[1, i, cut], {"dp": partner},
        )

    for i in range(LINE):
        for cut in range(CUTS):
            pre_copy(i, cut).start()

    def own_copy(i):
        return pltpu.make_async_copy(
            pre_hbm.at[:, columns(order(i), x)], pre_own.at[i], local_sems.at[i]
        )

    for i in range(LINE):
        own_copy(i).start()
    weight_own = pltpu.make_async_copy(weight_hbm, weights.at[z], local_sems.at[LINE])
    weight_own.start()

    def slots(source):
        return pl.ds(pl.multiple_of(source * capacity, capacity), capacity)

    def arrival(rep, k):
        source = lax.rem(me + experts - k, experts)
        return remote(
            outgoing.at[rep, k - 1],
            arrived.at[rep, slots(source)],
            send_sems.at[rep, k - 1],
            arrive_sems.at[rep, k - 1],
            {"expert": lax.rem(me + k, experts)},
        )

    earlier = (
        lax.broadcasted_iota(jnp.int32, (count, count), 0)
        < lax.broadcasted_iota(jnp.int32, (count, count), 1)
    ).astype(jnp.float32).astype(jnp.bfloat16)

    def dispatch(rep, routes, tokens):
        names = routes[...]
        named = lax.broadcasted_iota(jnp.int32, (8, count), 0) == names
        onehot = named.astype(jnp.float32)
        before = jnp.dot(
            onehot.astype(jnp.bfloat16), earlier, preferred_element_type=jnp.float32
        )
        position = jnp.sum(onehot * before, axis=0, keepdims=True).astype(jnp.int32)
        slot = lax.broadcasted_iota(jnp.int32, (capacity, count), 0)
        for k in list(range(1, experts)) + [0]:
            target = lax.rem(me + k, experts)
            place = jnp.where(names == target, position, -1)
            choose = (slot == place).astype(jnp.float32).astype(jnp.bfloat16)
            rows_out = jnp.dot(
                choose, tokens[...], preferred_element_type=jnp.float32
            ).astype(jnp.bfloat16)
            if k == 0:
                arrived[rep, slots(me), :] = rows_out
            else:
                outgoing[rep, k - 1] = rows_out
                remote(
                    outgoing.at[rep, k - 1],
                    arrived.at[rep, slots(me)],
                    send_sems.at[rep, k - 1],
                    arrive_sems.at[rep, k - 1],
                    {"expert": target},
                ).start()

    dispatch(0, route_ref, tokens_ref)

    strip = 64

    def activate_rows(rep, i, source, cut):
        at_columns = within(cut)

        @pl.loop(0, rows // (2 * strip))
        def _(t):
            for half in range(2):
                at = pl.ds(pl.multiple_of(t * 2 * strip + half * strip, strip), strip)
                v = source[i, at, at_columns].astype(jnp.float32)
                square = v * v
                tangent = jnp.tanh(tanh_scale * v * (1.0 + cubic_weight * square))
                gate = 0.5 * (1.0 + tangent)
                slope[rep, i, at, at_columns] = gate + 0.5 * v * (
                    1.0 - tangent * tangent
                ) * tanh_scale * (1.0 + 3.0 * cubic_weight * square)
                hidden[rep, i, at, at_columns] = (v * gate).astype(jnp.bfloat16)

    route_copy.wait_recv()
    token_copy.wait_recv()
    dispatch(1, their_route, their_tokens)
    for i in range(LINE):
        own_copy(i).wait()

        @pl.loop(0, CUTS)
        def _(cut):
            activate_rows(0, i, pre_own, cut)

    weight_arrive(0)
    weight_start(1)
    for rep in range(2):
        for k in range(1, experts):
            arrival(rep, k).wait_recv()

    tile = 256

    def multiply(i):
        @pl.loop(0, CUTS)
        def _(cut):
            pre_copy(i, cut).wait_recv()
            activate_rows(1, i, pre_theirs, cut)
            at = within(cut)
            total = lax.dot_general(
                hidden[0, i, :, at], arrived[0], (((0,), (0,)), ((), ())),
                preferred_element_type=jnp.float32,
            )
            partial[i, at, :] = total + lax.dot_general(
                hidden[1, i, :, at], arrived[1], (((0,), (0,)), ((), ())),
                preferred_element_type=jnp.float32,
            )
            if i < LINE - 1:
                pass_on(i, True, cut)

    def sum_copy(direction, stage, cut):
        part = within(cut)
        return remote(
            sums_out.at[direction, stage, part], sums_in.at[direction, stage, part],
            sum_send.at[direction, stage, cut], sum_recv.at[direction, stage, cut],
            {"dp": d + (1 - 2 * direction) * PAIR},
        )

    def pass_on(i, ends, cut):
        j = order(i)
        part = within(cut)
        for direction in range(2):
            distance = (j - z) if direction == 0 else (z - j)
            first = (z == 0) if direction == 0 else (z == LINE - 1)
            stage = jnp.clip(LINE - 1 - distance, 0, LINE - 2)
            if ends:
                @pl.when((distance > 0) & first)
                def _():
                    sums_out[direction, stage, part, :] = partial[i, part, :].astype(
                        jnp.bfloat16
                    )
                    sum_copy(direction, stage, cut).start()
            else:
                @pl.when((distance > 0) & jnp.logical_not(first))
                def _():
                    last = jnp.clip(stage - 1, 0, LINE - 2)
                    sum_copy(direction, last, cut).wait_recv()
                    sums_out[direction, stage, part, :] = (
                        partial[i, part, :]
                        + sums_in[direction, last, part, :].astype(jnp.float32)
                    ).astype(jnp.bfloat16)
                    sum_copy(direction, stage, cut).start()

    def forward(*blocks):
        @pl.loop(0, CUTS)
        def _(cut):
            for i in blocks:
                pass_on(i, False, cut)

    def grad_copy(i):
        return remote(
            pre_theirs.at[i], grad_hbm.at[:, columns(order(i), x)],
            grad_sems.at[0, i], grad_sems.at[1, i], {"dp": partner},
        )

    def grad_arrive(i):
        return remote(
            pre_theirs.at[i], grad_hbm.at[:, columns(order(i), 1 - x)],
            grad_sems.at[0, i], grad_sems.at[1, i], {"dp": partner},
        )

    def grad_write(i):
        return pltpu.make_async_copy(
            pre_own.at[i], grad_hbm.at[:, columns(order(i), x)], grad_sems.at[2, i]
        )

    def differentiate(i):
        j = order(i)
        for rep, result in ((1, pre_theirs), (0, pre_own)):
            @pl.loop(0, rows // tile)
            def _(t):
                at = pl.ds(pl.multiple_of(t * tile, tile), tile)
                product = lax.dot_general(
                    arrived[rep, at, :], weights[j], (((1,), (1,)), ((), ())),
                    preferred_element_type=jnp.float32,
                )
                result[i, at, :] = (product * slope[rep, i, at, :]).astype(jnp.bfloat16)

            if rep == 1:
                grad_copy(i).start()
            else:
                grad_write(i).start()

    multiply(0)
    multiply(1)
    weight_arrive(1)
    weight_start(2)
    weight_own.wait()
    forward(0)
    multiply(2)
    differentiate(2)
    differentiate(1)
    multiply(3)
    differentiate(3)
    weight_arrive(2)
    differentiate(0)
    forward(1, 2)

    def result_copy(cut):
        part = pl.ds(cut * piece, piece)
        return pltpu.make_async_copy(
            partial.at[LINE - 1, part], dw_hbm.at[part], local_sems.at[LINE + 1 + cut]
        )

    for cut in range(CUTS):
        part = pl.ds(cut * piece, piece)
        for direction in range(2):
            @pl.when(receives(direction, 0))
            def _():
                sum_copy(direction, LINE - 2, cut).wait_recv()
                partial[LINE - 1, part, :] += sums_in[direction, LINE - 2, part, :].astype(jnp.float32)
        partial[LINE - 1, part, :] = partial[LINE - 1, part, :] * factor
        result_copy(cut).start()

    for i in range(LINE):
        grad_arrive(i).wait_recv()
        grad_write(i).wait()
    for cut in range(CUTS):
        result_copy(cut).wait()
    route_copy.wait_send()
    token_copy.wait_send()
    for i in range(LINE):
        for cut in range(CUTS):
            pre_copy(i, cut).wait_send()
        grad_copy(i).wait_send()
    for rep in range(2):
        for k in range(1, experts):
            arrival(rep, k).wait_send()
    for hop in range(LINE - 1):
        for direction in range(2):
            @pl.when(sends(direction, hop))
            def _():
                weight_copy(direction, hop).wait_send()
    for stage in range(LINE - 1):
        for direction in range(2):
            toward = (z <= stage) if direction == 0 else (z >= LINE - 1 - stage)
            inside = (z < LINE - 1) if direction == 0 else (z > 0)

            @pl.when(toward & inside)
            def _():
                for cut in range(CUTS):
                    sum_copy(direction, stage, cut).wait_send()


def fused(out_grad, expert_of, pre_act, down_weight):
    experts = lax.axis_size("expert")
    replicas = lax.axis_size("dp")
    count, width = out_grad.shape
    rows, units = pre_act.shape
    block = down_weight.shape[1]
    capacity = count // 2
    factor = 1.0 / math.sqrt(replicas * count)
    half, full = jnp.bfloat16, jnp.float32
    vmem = pl.BlockSpec(memory_space=pltpu.VMEM)
    anywhere = pl.BlockSpec(memory_space=pl.ANY)
    dma = pltpu.SemaphoreType.DMA
    pre_grad, summed = pl.pallas_call(
        functools.partial(kernel, experts, capacity, factor),
        out_shape=(
            jax.ShapeDtypeStruct((rows, units), half),
            jax.ShapeDtypeStruct((block, width), full),
        ),
        in_specs=[vmem, vmem, anywhere, anywhere],
        out_specs=(anywhere, anywhere),
        scratch_shapes=[
            pltpu.VMEM((count, width), half),
            pltpu.VMEM((1, count), jnp.int32),
            pltpu.VMEM((2, experts - 1, capacity, width), half),
            pltpu.VMEM((2, rows, width), half),
            pltpu.VMEM((LINE, rows, block), half),
            pltpu.VMEM((LINE, rows, block), half),
            pltpu.VMEM((LINE, block, width), half),
            pltpu.VMEM((2, LINE, rows, block), half),
            pltpu.VMEM((2, LINE, rows, block), full),
            pltpu.VMEM((LINE, block, width), full),
            pltpu.VMEM((2, LINE - 1, block, width), half),
            pltpu.VMEM((2, LINE - 1, block, width), half),
            dma((4,)),
            dma((2, experts - 1)),
            dma((2, experts - 1)),
            dma((LINE + 1 + CUTS,)),
            dma((2, LINE, CUTS)),
            dma((2, LINE - 1)),
            dma((2, LINE - 1)),
            dma((2, LINE - 1, CUTS)),
            dma((2, LINE - 1, CUTS)),
            dma((3, LINE)),
        ],
        compiler_params=pltpu.CompilerParams(
            collective_id=0, has_side_effects=True, vmem_limit_bytes=46 * 1024 * 1024
        ),
    )(out_grad, expert_of.reshape(1, count), pre_act, down_weight[0])
    return pre_grad, summed.reshape(1, block, width)


def body(out_grad, expert_of, pre_act, down_weight):
    experts = lax.axis_size("expert")
    replicas = lax.axis_size("dp")
    if replicas == PAIR * LINE and experts <= 8:
        return fused(out_grad, expert_of, pre_act, down_weight)
    token_count = out_grad.shape[0]
    model_width = out_grad.shape[1]
    capacity = token_count // 2
    routed = expert_of[:, 0]
    onehot = (routed[:, None] == jnp.arange(experts, dtype=jnp.int32)[None, :]).astype(jnp.int32)
    position = jnp.sum((jnp.cumsum(onehot, axis=0) - onehot) * onehot, axis=1)
    target = routed * capacity + position
    outgoing = jnp.zeros((experts * capacity, model_width), jnp.bfloat16).at[target].set(out_grad)
    arrived = lax.all_to_all(
        outgoing.reshape(experts, capacity, model_width),
        "expert",
        split_axis=0,
        concat_axis=0,
        tiled=True,
    )
    arrived = arrived.reshape(experts * capacity, model_width)
    weight = down_weight[0]
    own_rows = weight.shape[0]
    factor = 1.0 / math.sqrt(replicas * token_count)
    hidden_grad = lax.dot_general(
        arrived,
        lax.all_gather(weight, "dp", axis=0, tiled=True),
        (((1,), (1,)), ((), ())),
        preferred_element_type=jnp.float32,
    )
    pre_block = pre_act.astype(jnp.float32)
    pre_grad = (hidden_grad * derivative(pre_block)).astype(jnp.bfloat16)
    hidden = activate(pre_block).astype(jnp.bfloat16)
    summed = lax.psum_scatter(
        lax.dot_general(
            hidden, arrived, (((0,), (0,)), ((), ())), preferred_element_type=jnp.float32
        ),
        "dp",
        scatter_dimension=0,
        tiled=True,
    )
    return (pre_grad, (summed * factor).reshape(1, own_rows, model_width))


def solution(mesh):
    placed = (
        P(("dp", "expert"), None),
        P(("dp", "expert"), None),
        P(("dp", "expert"), None),
        P("expert", "dp", None),
    )
    return jax.shard_map(
        body,
        mesh=mesh,
        in_specs=placed,
        out_specs=(P(("dp", "expert"), None), P("expert", "dp", None)),
        check_vma=False,
    )
```

profile of v0, /device:TPU:0, one launch (start us, length us, event | category | flops | bytes accessed | tf_op | source)
XLA Modules:
  0.0 114.4 jit_solution(11293474382872154281)
XLA Ops:
  0.6 0.0 copy-start
  0.6 1.2 %copy-done = bf16[1,512,1024]{2,1,0:T(8,128)(2,1)S(1)} copy-done((bf16[1,512,1024]{2,1,0:T(8,128)(2,1)S(1)}, bf16[1,512,1024]{2,1,0:T(8,128)(2,1)}, u32[]{:S(2)}) %copy-start) | copy-done | bytes 1048600
  1.9 0.0 copy-start.1
  1.9 1.0 copy-done.1
  2.9 0.0 copy-start.2
  2.9 0.7 copy-done.2
  3.6 107.4 %shard_map.59 = (bf16[512,4096]{1,0:T(8,128)(2,1)S(1)}, f32[512,1024]{1,0:T(8,128)S(1)}) custom-call(bf16[256,1024]{1,0:T(8,128)(2,1)S(1)} %copy-done.1, s32[1,256]{1,0:T(1,128)S(1)} %bitcast.5, bf16[512,4096]{1,0:T(8,128)(2,1)} %pre_hbm.1, bf16[512,1024]{1,0:T(8,128)(2,1)S(1)} %bitcast.4), custom_call_target="tpu_custom_call" | custom-call | tf_op jit(solution)/shard_map/pallas_call | solution.py:429
  111.0 2.0 %copy.8 = bf16[512,4096]{1,0:T(8,128)(2,1)} copy(bf16[512,4096]{1,0:T(8,128)(2,1)S(1)} %get-tuple-element.8) | data formatting | bytes 8388608
  113.0 1.3 %copy.9 = f32[1,512,1024]{2,1,0:T(8,128)} copy(f32[1,512,1024]{2,1,0:T(8,128)S(1)} %bitcast.3) | data formatting | bytes 4194304
Async XLA Ops:
  0.6 1.2 %copy-start = (bf16[1,512,1024]{2,1,0:T(8,128)(2,1)S(1)}, bf16[1,512,1024]{2,1,0:T(8,128)(2,1)}, u32[]{:S(2)}) copy-start(bf16[1,512,1024]{2,1,0:T(8,128)(2,1)} %param.7) | copy-start | bytes 3145732
  1.9 1.0 copy-start.1
  2.9 0.7 copy-start.2
where the time goes:
time: 115 us; the launch traced here: 114 us
  Pallas kernels  107 us (93%)
  local copies, waits for them, and re-layouts  6.27 us (5%)
    pallas_call x1, Pallas kernels, fused(): pl.pallas_call(functools.partial(kernel, experts, capacity, factor), out_...  107 us
    unnamed x8, local copies, waits for them, and re-layouts  6.27 us

commit v1 on v0

--- a/solution.py
+++ b/solution.py
@@ -32,12 +32,14 @@
     experts,
     capacity,
     factor,
-    tokens_ref,
-    route_ref,
+    tokens_hbm,
+    route_hbm,
     pre_hbm,
     weight_hbm,
     grad_hbm,
     dw_hbm,
+    tokens_ref,
+    route_ref,
     their_tokens,
     their_route,
     outgoing,
@@ -50,6 +52,7 @@
     partial,
     sums_out,
     sums_in,
+    input_sems,
     token_sems,
     send_sems,
     arrive_sems,
@@ -87,6 +90,11 @@
     def within(cut):
         return pl.ds(pl.multiple_of(cut * piece, piece), piece)
 
+    route_load = pltpu.make_async_copy(route_hbm, route_ref, input_sems.at[0])
+    token_load = pltpu.make_async_copy(tokens_hbm, tokens_ref, input_sems.at[1])
+    route_load.start()
+    token_load.start()
+
     barrier = pltpu.get_barrier_semaphore()
     pl.semaphore_signal(barrier, inc=1, device_id={"dp": partner}, device_id_type=MESH)
     for k in range(1, experts):
@@ -112,10 +120,10 @@
         )
 
     route_copy = remote(
-        route_ref, their_route, token_sems.at[0], token_sems.at[1], {"dp": partner}
+        route_hbm, their_route, token_sems.at[0], token_sems.at[1], {"dp": partner}
     )
     token_copy = remote(
-        tokens_ref, their_tokens, token_sems.at[2], token_sems.at[3], {"dp": partner}
+        tokens_hbm, their_tokens, token_sems.at[2], token_sems.at[3], {"dp": partner}
     )
     route_copy.start()
     token_copy.start()
@@ -225,6 +233,8 @@
                     {"expert": target},
                 ).start()
 
+    route_load.wait()
+    token_load.wait()
     dispatch(0, route_ref, tokens_ref)
 
     strip = 64
@@ -423,7 +433,7 @@
     capacity = count // 2
     factor = 1.0 / math.sqrt(replicas * count)
     half, full = jnp.bfloat16, jnp.float32
-    vmem = pl.BlockSpec(memory_space=pltpu.VMEM)
+    hbm = pl.BlockSpec(memory_space=pltpu.HBM)
     anywhere = pl.BlockSpec(memory_space=pl.ANY)
     dma = pltpu.SemaphoreType.DMA
     pre_grad, summed = pl.pallas_call(
@@ -432,9 +442,11 @@
             jax.ShapeDtypeStruct((rows, units), half),
             jax.ShapeDtypeStruct((block, width), full),
         ),
-        in_specs=[vmem, vmem, anywhere, anywhere],
+        in_specs=[hbm, hbm, hbm, hbm],
         out_specs=(anywhere, anywhere),
         scratch_shapes=[
+            pltpu.VMEM((count, width), half),
+            pltpu.VMEM((1, count), jnp.int32),
             pltpu.VMEM((count, width), half),
             pltpu.VMEM((1, count), jnp.int32),
             pltpu.VMEM((2, experts - 1, capacity, width), half),
@@ -447,6 +459,7 @@
             pltpu.VMEM((LINE, block, width), full),
             pltpu.VMEM((2, LINE - 1, block, width), half),
             pltpu.VMEM((2, LINE - 1, block, width), half),
+            dma((2,)),
             dma((4,)),
             dma((2, experts - 1)),
             dma((2, experts - 1)),
@@ -461,7 +474,10 @@
         compiler_params=pltpu.CompilerParams(
             collective_id=0, has_side_effects=True, vmem_limit_bytes=46 * 1024 * 1024
         ),
-    )(out_grad, expert_of.reshape(1, count), pre_act, down_weight[0])
+    )(*(
+        pltpu.with_memory_space_constraint(array, pltpu.HBM)
+        for array in (out_grad, expert_of.reshape(1, count), pre_act, down_weight[0])
+    ))
     return pre_grad, summed.reshape(1, block, width)
 
 

time: 115 us -> 112 us (0.974)
  local copies, waits for them, and re-layouts: 6.27 us -> 3.33 us
    unnamed x8 -> x2, local copies, waits for them, and re-layouts: 6.27 us -> 3.33 us
where the time goes in v1:
time: 112 us
  Pallas kernels  108 us (96%)
  local copies, waits for them, and re-layouts  3.33 us (3%)
    pallas_call x1, Pallas kernels, fused(): pl.pallas_call(functools.partial(kernel, experts, capacity, factor), out_...  108 us
    unnamed x2, local copies, waits for them, and re-layouts  3.33 us

profile of v1, /device:TPU:0, one launch (start us, length us, event | category | flops | bytes accessed | tf_op | source)
XLA Modules:
  0.0 111.7 jit_solution(14217927587271177654)
XLA Ops:
  0.6 107.7 %shard_map.59 = (bf16[512,4096]{1,0:T(8,128)(2,1)S(1)}, f32[512,1024]{1,0:T(8,128)S(1)}) custom-call(bf16[256,1024]{1,0:T(8,128)(2,1)} %tokens_hbm.1, s32[1,256]{1,0:T(1,128)} %bitcast.5, bf16[512,4096]{1,0:T(8,128)(2,1)} %pre_hbm.1, bf16[512,1024]{1,0:T(8,128)(2,1)} %bitcast.4), custom_call_target="tpu_custom_call" | custom-call | tf_op jit(solution)/shard_map/pallas_call | solution.py:439
  108.4 2.0 %copy.8 = bf16[512,4096]{1,0:T(8,128)(2,1)} copy(bf16[512,4096]{1,0:T(8,128)(2,1)S(1)} %get-tuple-element.8) | data formatting | bytes 8388608
  110.4 1.3 %copy.9 = f32[1,512,1024]{2,1,0:T(8,128)} copy(f32[1,512,1024]{2,1,0:T(8,128)S(1)} %bitcast.3) | data formatting | bytes 4194304

commit v2 on v1

v2 whole, which is shorter than its diff:
```python
import functools
import math

import jax
import jax.numpy as jnp
from jax import lax
from jax.experimental import pallas as pl
from jax.experimental.pallas import tpu as pltpu
from jax.sharding import PartitionSpec as P

tanh_scale = 0.7978845608028654
cubic_weight = 0.044715
MESH = pl.DeviceIdType.MESH
PAIR = 2
LINE = 4
CUTS = 2
HALVES = 2
PARTS = 4


def activate(values):
    argument = tanh_scale * (values + cubic_weight * values * values * values)
    return 0.5 * values * (1.0 + jnp.tanh(argument))


def derivative(values):
    tangent = jnp.tanh(tanh_scale * (values + cubic_weight * values * values * values))
    return 0.5 * (1.0 + tangent) + 0.5 * values * (1.0 - tangent * tangent) * tanh_scale * (
        1.0 + 3.0 * cubic_weight * values * values
    )


def kernel(
    experts,
    capacity,
    factor,
    tokens_hbm,
    route_hbm,
    pre_hbm,
    weight_hbm,
    grad_hbm,
    dw_hbm,
    own_tokens,
    own_route,
    their_tokens,
    their_route,
    choose,
    outgoing,
    arrived,
    pre_own,
    pre_theirs,
    lane_in,
    lane_pack,
    lane_got,
    lane_out,
    weights,
    hidden,
    slope,
    partial,
    sums_out,
    sums_in,
    input_sems,
    token_sems,
    dispatch_send,
    dispatch_recv,
    local_sems,
    pre_sems,
    lane_send,
    lane_recv,
    cross_sems,
    weight_send,
    weight_recv,
    sum_send,
    sum_recv,
    grad_sems,
):
    d = lax.axis_index("dp")
    me = lax.axis_index("expert")
    z = lax.div(d, PAIR)
    x = lax.rem(d, PAIR)
    partner = z * PAIR + 1 - x
    rows, width = pre_hbm.shape[0], own_tokens.shape[1]
    block = weight_hbm.shape[0]
    count = own_tokens.shape[0]
    low = z < LINE // 2
    own = LINE - 1
    piece, part_rows, span = block // CUTS, block // PARTS, width // HALVES
    chunks = [(cut, half) for half in range(HALVES) for cut in range(CUTS)]

    def order(i):
        if i == own:
            return z
        down = LINE - 1 - i
        return jnp.where(
            low, jnp.where(down > z, down, down - 1), jnp.where(i < z, i, i + 1)
        )

    def columns(j, side):
        return pl.ds(pl.multiple_of((j * PAIR + side) * block, block), block)

    def within(cut):
        return pl.ds(cut * piece, piece)

    def across(half):
        return pl.ds(half * span, span)

    def slots(source):
        return pl.ds(pl.multiple_of(source * capacity, capacity), capacity)

    def peer(k):
        return lax.rem(me + k, experts)

    def from_peer(k):
        return lax.rem(me + experts - k, experts)

    route_load = pltpu.make_async_copy(route_hbm, own_route, input_sems.at[0])
    token_load = pltpu.make_async_copy(tokens_hbm, own_tokens, input_sems.at[1])
    route_load.start()
    token_load.start()

    barrier = pltpu.get_barrier_semaphore()
    pl.semaphore_signal(barrier, inc=1, device_id={"dp": partner}, device_id_type=MESH)
    for k in range(1, experts):
        pl.semaphore_signal(
            barrier, inc=1, device_id={"expert": peer(k)}, device_id_type=MESH
        )

    @pl.when(z > 0)
    def _():
        pl.semaphore_signal(barrier, inc=1, device_id={"dp": d - PAIR}, device_id_type=MESH)

    @pl.when(z < LINE - 1)
    def _():
        pl.semaphore_signal(barrier, inc=1, device_id={"dp": d + PAIR}, device_id_type=MESH)

    inner = jnp.where((z > 0) & (z < LINE - 1), 2, 1)
    pl.semaphore_wait(barrier, experts + inner)

    def remote(src, dst, send, recv, device):
        return pltpu.make_async_remote_copy(
            src_ref=src, dst_ref=dst, send_sem=send, recv_sem=recv,
            device_id=device, device_id_type=MESH,
        )

    route_copy = remote(
        route_hbm, their_route, token_sems.at[0, HALVES], token_sems.at[1, HALVES],
        {"dp": partner},
    )

    def token_copy(half):
        return remote(
            tokens_hbm.at[:, across(half)], their_tokens.at[:, across(half)],
            token_sems.at[0, half], token_sems.at[1, half], {"dp": partner},
        )

    def pre_copy(i, cut):
        start = (order(i) * PAIR + 1 - x) * block + cut * piece
        return remote(
            pre_hbm.at[:, pl.ds(pl.multiple_of(start, piece), piece)],
            pre_theirs.at[i, :, within(cut)],
            pre_sems.at[0, i, cut], pre_sems.at[1, i, cut], {"dp": partner},
        )

    def cross(lane):
        return remote(
            lane_pack.at[lane], lane_got.at[lane],
            cross_sems.at[0, lane], cross_sems.at[1, lane], {"dp": partner},
        )

    def part(c):
        return pl.ds(c * part_rows, part_rows)

    def weight_copy(direction, hop, c):
        step = 1 - 2 * direction
        shard = jnp.clip(z - step * hop, 0, LINE - 1)
        src = weight_hbm if hop == 0 else weights.at[shard]
        return remote(
            src.at[part(c)], weights.at[shard, part(c)], weight_send.at[direction, hop, c],
            weight_recv.at[direction, hop, c], {"dp": d + step * PAIR},
        )

    def sends(direction, hop):
        if direction == 0:
            return (z >= hop) & (z < LINE - 1)
        return (z <= LINE - 1 - hop) & (z > 0)

    def receives(direction, hop):
        return (z > hop) if direction == 0 else (z < LINE - 1 - hop)

    def weight_start(hop, c):
        for direction in range(2):
            @pl.when(sends(direction, hop))
            def _():
                weight_copy(direction, hop, c).start()

    def weight_arrive(hop, c):
        for direction in range(2):
            @pl.when(receives(direction, hop))
            def _():
                step = 1 - 2 * direction
                shard = jnp.clip(z - step * (hop + 1), 0, LINE - 1)
                remote(
                    weight_hbm.at[part(c)], weights.at[shard, part(c)],
                    weight_send.at[direction, hop, c],
                    weight_recv.at[direction, hop, c], {"dp": partner},
                ).wait_recv()

        if hop < LINE - 2:
            weight_start(hop + 1, c)

    route_copy.start()
    for half in range(HALVES):
        token_copy(half).start()
    for c in range(PARTS):
        weight_start(0, c)
    for i in range(own - 1):
        for cut in range(CUTS):
            pre_copy(i, cut).start()

    def own_copy(i):
        return pltpu.make_async_copy(
            pre_hbm.at[:, columns(order(i), x)], pre_own.at[i], local_sems.at[i]
        )

    for i in range(LINE):
        own_copy(i).start()
    weight_own = pltpu.make_async_copy(weight_hbm, weights.at[z], local_sems.at[LINE])
    weight_own.start()

    earlier = (
        lax.broadcasted_iota(jnp.int32, (count, count), 0)
        < lax.broadcasted_iota(jnp.int32, (count, count), 1)
    ).astype(jnp.float32).astype(jnp.bfloat16)

    def plan(rep, routes):
        names = routes[...]
        named = lax.broadcasted_iota(jnp.int32, (8, count), 0) == names
        onehot = named.astype(jnp.float32)
        before = jnp.dot(
            onehot.astype(jnp.bfloat16), earlier, preferred_element_type=jnp.float32
        )
        position = jnp.sum(onehot * before, axis=0, keepdims=True).astype(jnp.int32)
        slot = lax.broadcasted_iota(jnp.int32, (capacity, count), 0)
        for e in range(experts):
            place = jnp.where(names == e, position, -1)
            choose[rep, e * capacity:(e + 1) * capacity, :] = (
                (slot == place).astype(jnp.float32).astype(jnp.bfloat16)
            )

    def dispatch_copy(rep, k, half):
        return remote(
            outgoing.at[rep, k - 1, :, across(half)],
            arrived.at[rep, slots(me), across(half)],
            dispatch_send.at[rep, k - 1, half],
            dispatch_recv.at[rep, k - 1, half],
            {"expert": peer(k)},
        )

    def dispatch(rep, tokens, half):
        for k in list(range(1, experts)) + [0]:
            rows_out = jnp.dot(
                choose[rep, slots(peer(k)), :], tokens[:, across(half)],
                preferred_element_type=jnp.float32,
            ).astype(jnp.bfloat16)
            if k == 0:
                arrived[rep, slots(me), across(half)] = rows_out
            else:
                outgoing[rep, k - 1, :, across(half)] = rows_out
                dispatch_copy(rep, k, half).start()

    def tokens_arrive(rep, half):
        for k in range(1, experts):
            remote(
                outgoing.at[rep, k - 1, :, across(half)],
                arrived.at[rep, slots(from_peer(k)), across(half)],
                dispatch_send.at[rep, k - 1, half],
                dispatch_recv.at[rep, k - 1, half],
                {"expert": peer(k)},
            ).wait_recv()

    def lane_copy(leg, k):
        target = peer(k)
        if leg == 0:
            src = pre_hbm.at[slots(target), columns(z, 1 - x)]
            dst = lane_in.at[0, slots(me)]
        elif leg == 1:
            src = lane_out.at[0, k - 1]
            dst = pre_theirs.at[own, slots(me)]
        elif leg == 2:
            src = pre_theirs.at[own, slots(target)]
            dst = lane_in.at[1, slots(me)]
        else:
            src = lane_out.at[1, k]
            dst = grad_hbm.at[slots(me), columns(z, 1 - x)]
        return remote(
            src, dst, lane_send.at[leg, k - 1], lane_recv.at[leg, k - 1], {"expert": target}
        )

    def lane_arrive(leg):
        for k in range(1, experts):
            source = from_peer(k)
            if leg == 0:
                dst = lane_in.at[0, slots(source)]
            elif leg == 1:
                dst = pre_theirs.at[own, slots(source)]
            elif leg == 2:
                dst = lane_in.at[1, slots(source)]
            else:
                dst = grad_hbm.at[slots(source), columns(z, 1 - x)]
            remote(
                lane_out.at[0, k - 1], dst, lane_send.at[leg, k - 1], lane_recv.at[leg, k - 1],
                {"expert": peer(k)},
            ).wait_recv()

    lane_local = pltpu.make_async_copy(
        pre_hbm.at[slots(me), columns(z, 1 - x)], lane_in.at[0, slots(me)],
        local_sems.at[LINE + 1],
    )
    lane_home = pltpu.make_async_copy(
        lane_out.at[1, 0], grad_hbm.at[slots(me), columns(z, 1 - x)], local_sems.at[LINE + 2]
    )

    def gather(lane):
        lane_pack[lane] = lax.dot_general(
            choose[lane], lane_in[lane], (((0,), (0,)), ((), ())),
            preferred_element_type=jnp.float32,
        ).astype(jnp.bfloat16)
        cross(lane).start()

    def spread(lane):
        cross(lane).wait_recv()
        for k in list(range(1, experts)) + [0]:
            rows_out = jnp.dot(
                choose[1 - lane, slots(peer(k)), :], lane_got[lane],
                preferred_element_type=jnp.float32,
            ).astype(jnp.bfloat16)
            if lane == 0:
                if k == 0:
                    pre_theirs[own, slots(me), :] = rows_out
                else:
                    lane_out[0, k - 1] = rows_out
                    lane_copy(1, k).start()
            else:
                lane_out[1, k] = rows_out
                if k == 0:
                    lane_home.start()
                else:
                    lane_copy(3, k).start()

    strip = 64

    def activate_rows(rep, i, source, cut):
        at_columns = within(cut)

        @pl.loop(0, rows // (2 * strip))
        def _(t):
            for half in range(2):
                at = pl.ds(pl.multiple_of(t * 2 * strip + half * strip, strip), strip)
                v = source[i, at, at_columns].astype(jnp.float32)
                square = v * v
                tangent = jnp.tanh(tanh_scale * v * (1.0 + cubic_weight * square))
                gate = 0.5 * (1.0 + tangent)
                slope[rep, i, at, at_columns] = gate + 0.5 * v * (
                    1.0 - tangent * tangent
                ) * tanh_scale * (1.0 + 3.0 * cubic_weight * square)
                hidden[rep, i, at, at_columns] = (v * gate).astype(jnp.bfloat16)

    def activate_own(i):
        own_copy(i).wait()
        for cut in range(CUTS):
            activate_rows(0, i, pre_own, cut)

    def activate_theirs(i, cut):
        if i < own:
            pre_copy(i, cut).wait_recv()
        activate_rows(1, i, pre_theirs, cut)

    def term(i, cut, half):
        at, wide = within(cut), across(half)
        total = lax.dot_general(
            hidden[0, i, :, at], arrived[0, :, wide], (((0,), (0,)), ((), ())),
            preferred_element_type=jnp.float32,
        )
        partial[i, at, wide] = total + lax.dot_general(
            hidden[1, i, :, at], arrived[1, :, wide], (((0,), (0,)), ((), ())),
            preferred_element_type=jnp.float32,
        )
        if i < own:
            pass_on(i, True, cut, half)

    def sum_copy(direction, stage, cut, half):
        at, wide = within(cut), across(half)
        return remote(
            sums_out.at[direction, stage, at, wide], sums_in.at[direction, stage, at, wide],
            sum_send.at[direction, stage, cut, half], sum_recv.at[direction, stage, cut, half],
            {"dp": d + (1 - 2 * direction) * PAIR},
        )

    def pass_on(i, ends, cut, half):
        j = order(i)
        at, wide = within(cut), across(half)
        for direction in range(2):
            distance = (j - z) if direction == 0 else (z - j)
            first = (z == 0) if direction == 0 else (z == LINE - 1)
            stage = jnp.clip(LINE - 1 - distance, 0, LINE - 2)
            if ends:
                @pl.when((distance > 0) & first)
                def _():
                    sums_out[direction, stage, at, wide] = partial[i, at, wide].astype(
                        jnp.bfloat16
                    )
                    sum_copy(direction, stage, cut, half).start()
            else:
                @pl.when((distance > 0) & jnp.logical_not(first))
                def _():
                    last = jnp.clip(stage - 1, 0, LINE - 2)
                    sum_copy(direction, last, cut, half).wait_recv()
                    sums_out[direction, stage, at, wide] = (
                        partial[i, at, wide]
                        + sums_in[direction, last, at, wide].astype(jnp.float32)
                    ).astype(jnp.bfloat16)
                    sum_copy(direction, stage, cut, half).start()

    def forward(i, chunk):
        pass_on(i, False, *chunk)

    def grad_copy(i):
        return remote(
            pre_theirs.at[i], grad_hbm.at[:, columns(order(i), x)],
            grad_sems.at[0, i], grad_sems.at[1, i], {"dp": partner},
        )

    def grad_arrive(i):
        return remote(
            pre_theirs.at[i], grad_hbm.at[:, columns(order(i), 1 - x)],
            grad_sems.at[0, i], grad_sems.at[1, i], {"dp": partner},
        )

    def grad_write(i):
        return pltpu.make_async_copy(
            pre_own.at[i], grad_hbm.at[:, columns(order(i), x)], grad_sems.at[2, i]
        )

    tile = 256

    def differentiate(rep, i):
        j = order(i)
        result = pre_theirs if rep == 1 else pre_own

        @pl.loop(0, rows // tile)
        def _(t):
            at = pl.ds(pl.multiple_of(t * tile, tile), tile)
            product = lax.dot_general(
                arrived[rep, at, :], weights[j], (((1,), (1,)), ((), ())),
                preferred_element_type=jnp.float32,
            )
            result[i, at, :] = (product * slope[rep, i, at, :]).astype(jnp.bfloat16)

        if rep == 0:
            grad_write(i).start()
        elif i < own:
            grad_copy(i).start()
        else:
            for k in range(1, experts):
                lane_copy(2, k).start()
            lane_in[1, slots(me), :] = pre_theirs[own, slots(me), :]

    route_load.wait()
    token_load.wait()
    plan(0, own_route)
    dispatch(0, own_tokens, 0)
    activate_own(0)
    activate_own(1)
    route_copy.wait_recv()
    plan(1, their_route)
    token_copy(0).wait_recv()
    dispatch(1, their_tokens, 0)
    dispatch(0, own_tokens, 1)
    activate_own(2)
    weight_arrive(0, 0)
    token_copy(1).wait_recv()
    dispatch(1, their_tokens, 1)
    lane_local.start()
    for k in range(1, experts):
        lane_copy(0, k).start()
    activate_own(own)
    weight_arrive(0, 1)
    for rep in range(2):
        tokens_arrive(rep, 0)
    activate_theirs(0, 0)
    term(0, 0, 0)
    weight_arrive(0, 2)
    activate_theirs(0, 1)
    term(0, 1, 0)
    weight_arrive(0, 3)
    for rep in range(2):
        tokens_arrive(rep, 1)
    term(0, 0, 1)
    term(0, 1, 1)
    weight_own.wait()
    differentiate(0, own)
    differentiate(0, own - 1)
    lane_local.wait()
    lane_arrive(0)
    gather(0)
    for cut in range(CUTS):
        pre_copy(own - 1, cut).start()
    weight_arrive(1, 0)
    forward(0, chunks[0])
    activate_theirs(1, 0)
    weight_arrive(1, 1)
    forward(0, chunks[1])
    activate_theirs(1, 1)
    for chunk in chunks:
        term(1, *chunk)
    weight_arrive(1, 2)
    forward(0, chunks[2])
    spread(0)
    weight_arrive(1, 3)
    forward(0, chunks[3])
    differentiate(1, 1)
    differentiate(0, 1)
    lane_arrive(1)
    for cut in range(CUTS):
        activate_theirs(own, cut)
    differentiate(1, own)
    for cut in range(CUTS):
        activate_theirs(2, cut)
    for chunk in chunks:
        term(2, *chunk)
    differentiate(1, 2)
    forward(1, chunks[0])
    forward(2, chunks[0])
    for chunk in chunks:
        term(own, *chunk)
    lane_arrive(2)
    gather(1)
    for c in range(2):
        weight_arrive(2, c)
    forward(1, chunks[1])
    forward(2, chunks[1])
    forward(1, chunks[2])
    forward(2, chunks[2])
    for c in range(2, PARTS):
        weight_arrive(2, c)
    differentiate(1, 0)
    forward(1, chunks[3])
    forward(2, chunks[3])
    differentiate(0, 0)

    def result_copy(cut, half):
        at, wide = within(cut), across(half)
        return pltpu.make_async_copy(
            partial.at[own, at, wide], dw_hbm.at[at, wide],
            local_sems.at[LINE + 3 + cut * HALVES + half],
        )

    for n, (cut, half) in enumerate(chunks):
        at, wide = within(cut), across(half)
        for direction in range(2):
            @pl.when(receives(direction, 0))
            def _():
                sum_copy(direction, LINE - 2, cut, half).wait_recv()
                partial[own, at, wide] += sums_in[direction, LINE - 2, at, wide].astype(
                    jnp.float32
                )
        partial[own, at, wide] = partial[own, at, wide] * factor
        result_copy(cut, half).start()
        if n == 1:
            spread(1)

    lane_arrive(3)
    lane_home.wait()
    for i in range(LINE):
        if i < own:
            grad_arrive(i).wait_recv()
        grad_write(i).wait()
    for cut, half in chunks:
        result_copy(cut, half).wait()
    route_copy.wait_send()
    for half in range(HALVES):
        token_copy(half).wait_send()
    for i in range(own):
        for cut in range(CUTS):
            pre_copy(i, cut).wait_send()
        grad_copy(i).wait_send()
    for lane in range(2):
        cross(lane).wait_send()
    for k in range(1, experts):
        for leg in range(4):
            lane_copy(leg, k).wait_send()
        for rep in range(2):
            for half in range(HALVES):
                dispatch_copy(rep, k, half).wait_send()
    for hop in range(LINE - 1):
        for direction in range(2):
            @pl.when(sends(direction, hop))
            def _():
                for c in range(PARTS):
                    weight_copy(direction, hop, c).wait_send()
    for stage in range(LINE - 1):
        for direction in range(2):
            toward = (z <= stage) if direction == 0 else (z >= LINE - 1 - stage)
            inside = (z < LINE - 1) if direction == 0 else (z > 0)

            @pl.when(toward & inside)
            def _():
                for cut, half in chunks:
                    sum_copy(direction, stage, cut, half).wait_send()


def fused(out_grad, expert_of, pre_act, down_weight):
    experts = lax.axis_size("expert")
    replicas = lax.axis_size("dp")
    count, width = out_grad.shape
    rows, units = pre_act.shape
    block = down_weight.shape[1]
    capacity = count // 2
    factor = 1.0 / math.sqrt(replicas * count)
    half, full = jnp.bfloat16, jnp.float32
    hbm = pl.BlockSpec(memory_space=pltpu.HBM)
    anywhere = pl.BlockSpec(memory_space=pl.ANY)
    dma = pltpu.SemaphoreType.DMA
    pre_grad, summed = pl.pallas_call(
        functools.partial(kernel, experts, capacity, factor),
        out_shape=(
            pltpu.VMEM((rows, units), half),
            pltpu.VMEM((block, width), full),
        ),
        in_specs=[hbm, hbm, hbm, hbm],
        out_specs=(anywhere, anywhere),
        scratch_shapes=[
            pltpu.VMEM((count, width), half),
            pltpu.VMEM((1, count), jnp.int32),
            pltpu.VMEM((count, width), half),
            pltpu.VMEM((1, count), jnp.int32),
            pltpu.VMEM((2, experts * capacity, count), half),
            pltpu.VMEM((2, experts - 1, capacity, width), half),
            pltpu.VMEM((2, rows, width), half),
            pltpu.VMEM((LINE, rows, block), half),
            pltpu.VMEM((LINE, rows, block), half),
            pltpu.VMEM((2, rows, block), half),
            pltpu.VMEM((2, count, block), half),
            pltpu.VMEM((2, count, block), half),
            pltpu.VMEM((2, experts, capacity, block), half),
            pltpu.VMEM((LINE, block, width), half),
            pltpu.VMEM((2, LINE, rows, block), half),
            pltpu.VMEM((2, LINE, rows, block), full),
            pltpu.VMEM((LINE, block, width), full),
            pltpu.VMEM((2, LINE - 1, block, width), half),
            pltpu.VMEM((2, LINE - 1, block, width), half),
            dma((2,)),
            dma((2, HALVES + 1)),
            dma((2, experts - 1, HALVES)),
            dma((2, experts - 1, HALVES)),
            dma((LINE + 3 + CUTS * HALVES,)),
            dma((2, LINE - 1, CUTS)),
            dma((4, experts - 1)),
            dma((4, experts - 1)),
            dma((2, 2)),
            dma((2, LINE - 1, PARTS)),
            dma((2, LINE - 1, PARTS)),
            dma((2, LINE - 1, CUTS, HALVES)),
            dma((2, LINE - 1, CUTS, HALVES)),
            dma((3, LINE)),
        ],
        compiler_params=pltpu.CompilerParams(
            collective_id=0, has_side_effects=True, vmem_limit_bytes=51 * 1024 * 1024
        ),
    )(*(
        pltpu.with_memory_space_constraint(array, pltpu.HBM)
        for array in (out_grad, expert_of.reshape(1, count), pre_act, down_weight[0])
    ))
    return pre_grad, summed.reshape(1, block, width)


def body(out_grad, expert_of, pre_act, down_weight):
    experts = lax.axis_size("expert")
    replicas = lax.axis_size("dp")
    if replicas == PAIR * LINE and experts <= 8:
        return fused(out_grad, expert_of, pre_act, down_weight)
    token_count = out_grad.shape[0]
    model_width = out_grad.shape[1]
    capacity = token_count // 2
    routed = expert_of[:, 0]
    onehot = (routed[:, None] == jnp.arange(experts, dtype=jnp.int32)[None, :]).astype(jnp.int32)
    position = jnp.sum((jnp.cumsum(onehot, axis=0) - onehot) * onehot, axis=1)
    target = routed * capacity + position
    outgoing = jnp.zeros((experts * capacity, model_width), jnp.bfloat16).at[target].set(out_grad)
    arrived = lax.all_to_all(
        outgoing.reshape(experts, capacity, model_width),
        "expert",
        split_axis=0,
        concat_axis=0,
        tiled=True,
    )
    arrived = arrived.reshape(experts * capacity, model_width)
    weight = down_weight[0]
    own_rows = weight.shape[0]
    factor = 1.0 / math.sqrt(replicas * token_count)
    hidden_grad = lax.dot_general(
        arrived,
        lax.all_gather(weight, "dp", axis=0, tiled=True),
        (((1,), (1,)), ((), ())),
        preferred_element_type=jnp.float32,
    )
    pre_block = pre_act.astype(jnp.float32)
    pre_grad = (hidden_grad * derivative(pre_block)).astype(jnp.bfloat16)
    hidden = activate(pre_block).astype(jnp.bfloat16)
    summed = lax.psum_scatter(
        lax.dot_general(
            hidden, arrived, (((0,), (0,)), ((), ())), preferred_element_type=jnp.float32
        ),
        "dp",
        scatter_dimension=0,
        tiled=True,
    )
    return (pre_grad, (summed * factor).reshape(1, own_rows, model_width))


def solution(mesh):
    placed = (
        P(("dp", "expert"), None),
        P(("dp", "expert"), None),
        P(("dp", "expert"), None),
        P("expert", "dp", None),
    )
    return jax.shard_map(
        body,
        mesh=mesh,
        in_specs=placed,
        out_specs=(P(("dp", "expert"), None), P("expert", "dp", None)),
        check_vma=False,
    )
```

time: 112 us -> 102 us (0.911)
  Pallas kernels: 108 us -> 97.8 us
    pallas_call x1, Pallas kernels: 108 us -> 97.8 us  [fused(): pl.pallas_call(functools.partial(kernel, experts, capacity, factor), out_...]
where the time goes in v2:
time: 102 us
  Pallas kernels  97.8 us (96%)
  local copies, waits for them, and re-layouts  3.33 us (3%)
    pallas_call x1, Pallas kernels, fused(): pl.pallas_call(functools.partial(kernel, experts, capacity, factor), out_...  97.8 us
    unnamed x2, local copies, waits for them, and re-layouts  3.33 us

profile of v2, /device:TPU:0, one launch (start us, length us, event | category | flops | bytes accessed | tf_op | source)
XLA Modules:
  0.0 101.7 jit_solution(12089701225709596649)
XLA Ops:
  0.6 97.8 %shard_map.59 = (bf16[512,4096]{1,0:T(8,128)(2,1)S(1)}, f32[512,1024]{1,0:T(8,128)S(1)}) custom-call(bf16[256,1024]{1,0:T(8,128)(2,1)} %tokens_hbm.1, s32[1,256]{1,0:T(1,128)} %bitcast.5, bf16[512,4096]{1,0:T(8,128)(2,1)} %pre_hbm.1, bf16[512,1024]{1,0:T(8,128)(2,1)} %bitcast.4), custom_call_target="tpu_custom_call" | custom-call | tf_op jit(solution)/shard_map/pallas_call | solution.py:624
  98.4 2.0 %copy.8 = bf16[512,4096]{1,0:T(8,128)(2,1)} copy(bf16[512,4096]{1,0:T(8,128)(2,1)S(1)} %get-tuple-element.6) | data formatting | bytes 8388608
  100.4 1.3 %copy.9 = f32[1,512,1024]{2,1,0:T(8,128)} copy(f32[1,512,1024]{2,1,0:T(8,128)S(1)} %bitcast.3) | data formatting | bytes 4194304

commit v3 on v2

--- a/solution.py
+++ b/solution.py
@@ -15,7 +15,8 @@
 LINE = 4
 CUTS = 2
 HALVES = 2
-PARTS = 4
+PARTS = 2
+LANES = 2
 
 
 def activate(values):
@@ -33,13 +34,13 @@
 def kernel(
     experts,
     capacity,
-    factor,
     tokens_hbm,
     route_hbm,
     pre_hbm,
     weight_hbm,
     grad_hbm,
-    dw_hbm,
+    term_out,
+    landed,
     own_tokens,
     own_route,
     their_tokens,
@@ -84,8 +85,8 @@
     count = own_tokens.shape[0]
     low = z < LINE // 2
     own = LINE - 1
+    direct = LINE - LANES
     piece, part_rows, span = block // CUTS, block // PARTS, width // HALVES
-    chunks = [(cut, half) for half in range(HALVES) for cut in range(CUTS)]
 
     def order(i):
         if i == own:
@@ -115,6 +116,8 @@
 
     route_load = pltpu.make_async_copy(route_hbm, own_route, input_sems.at[0])
     token_load = pltpu.make_async_copy(tokens_hbm, own_tokens, input_sems.at[1])
+    weight_own = pltpu.make_async_copy(weight_hbm, weights.at[z], local_sems.at[LINE])
+    weight_own.start()
     route_load.start()
     token_load.start()
 
@@ -149,7 +152,7 @@
 
     def token_copy(half):
         return remote(
-            tokens_hbm.at[:, across(half)], their_tokens.at[:, across(half)],
+            own_tokens.at[:, across(half)], their_tokens.at[:, across(half)],
             token_sems.at[0, half], token_sems.at[1, half], {"dp": partner},
         )
 
@@ -173,9 +176,8 @@
     def weight_copy(direction, hop, c):
         step = 1 - 2 * direction
         shard = jnp.clip(z - step * hop, 0, LINE - 1)
-        src = weight_hbm if hop == 0 else weights.at[shard]
-        return remote(
-            src.at[part(c)], weights.at[shard, part(c)], weight_send.at[direction, hop, c],
+        return remote(
+            weights.at[shard, part(c)], weights.at[shard, part(c)], weight_send.at[direction, hop, c],
             weight_recv.at[direction, hop, c], {"dp": d + step * PAIR},
         )
 
@@ -208,12 +210,14 @@
         if hop < LINE - 2:
             weight_start(hop + 1, c)
 
+    weight_own.wait()
+    for c in range(PARTS):
+        weight_start(0, c)
     route_copy.start()
+    token_load.wait()
     for half in range(HALVES):
         token_copy(half).start()
-    for c in range(PARTS):
-        weight_start(0, c)
-    for i in range(own - 1):
+    for i in range(direct):
         for cut in range(CUTS):
             pre_copy(i, cut).start()
 
@@ -224,9 +228,6 @@
 
     for i in range(LINE):
         own_copy(i).start()
-    weight_own = pltpu.make_async_copy(weight_hbm, weights.at[z], local_sems.at[LINE])
-    weight_own.start()
-
     earlier = (
         lax.broadcasted_iota(jnp.int32, (count, count), 0)
         < lax.broadcasted_iota(jnp.int32, (count, count), 1)
@@ -278,74 +279,80 @@
                 {"expert": peer(k)},
             ).wait_recv()
 
-    def lane_copy(leg, k):
-        target = peer(k)
+    def lane_unit(lane):
+        return own - lane
+
+    def lane_columns(lane):
+        return columns(order(lane_unit(lane)), 1 - x)
+
+    def lane_target(leg, lane, source):
         if leg == 0:
-            src = pre_hbm.at[slots(target), columns(z, 1 - x)]
-            dst = lane_in.at[0, slots(me)]
-        elif leg == 1:
-            src = lane_out.at[0, k - 1]
-            dst = pre_theirs.at[own, slots(me)]
+            return lane_in.at[lane, slots(source)]
+        if leg == 1:
+            return pre_theirs.at[lane_unit(lane), slots(source)]
+        if leg == 2:
+            return lane_in.at[LANES + lane, slots(source)]
+        return grad_hbm.at[slots(source), lane_columns(lane)]
+
+    def lane_copy(leg, lane, k):
+        if leg == 0:
+            src = pre_hbm.at[slots(peer(k)), lane_columns(lane)]
         elif leg == 2:
-            src = pre_theirs.at[own, slots(target)]
-            dst = lane_in.at[1, slots(me)]
+            src = pre_theirs.at[lane_unit(lane), slots(peer(k))]
         else:
-            src = lane_out.at[1, k]
-            dst = grad_hbm.at[slots(me), columns(z, 1 - x)]
-        return remote(
-            src, dst, lane_send.at[leg, k - 1], lane_recv.at[leg, k - 1], {"expert": target}
-        )
-
-    def lane_arrive(leg):
+            src = lane_out.at[lane + LANES * (leg // 2), k]
+        return remote(
+            src, lane_target(leg, lane, me), lane_send.at[leg, lane, k - 1],
+            lane_recv.at[leg, lane, k - 1], {"expert": peer(k)},
+        )
+
+    def lane_arrive(leg, lane):
         for k in range(1, experts):
-            source = from_peer(k)
-            if leg == 0:
-                dst = lane_in.at[0, slots(source)]
-            elif leg == 1:
-                dst = pre_theirs.at[own, slots(source)]
-            elif leg == 2:
-                dst = lane_in.at[1, slots(source)]
-            else:
-                dst = grad_hbm.at[slots(source), columns(z, 1 - x)]
             remote(
-                lane_out.at[0, k - 1], dst, lane_send.at[leg, k - 1], lane_recv.at[leg, k - 1],
+                lane_out.at[lane, k], lane_target(leg, lane, from_peer(k)),
+                lane_send.at[leg, lane, k - 1], lane_recv.at[leg, lane, k - 1],
                 {"expert": peer(k)},
             ).wait_recv()
 
-    lane_local = pltpu.make_async_copy(
-        pre_hbm.at[slots(me), columns(z, 1 - x)], lane_in.at[0, slots(me)],
-        local_sems.at[LINE + 1],
-    )
-    lane_home = pltpu.make_async_copy(
-        lane_out.at[1, 0], grad_hbm.at[slots(me), columns(z, 1 - x)], local_sems.at[LINE + 2]
-    )
-
-    def gather(lane):
-        lane_pack[lane] = lax.dot_general(
-            choose[lane], lane_in[lane], (((0,), (0,)), ((), ())),
+    def lane_local(lane):
+        return pltpu.make_async_copy(
+            pre_hbm.at[slots(me), lane_columns(lane)], lane_in.at[lane, slots(me)],
+            local_sems.at[LINE + 1 + lane],
+        )
+
+    def lane_home(lane):
+        return pltpu.make_async_copy(
+            lane_out.at[LANES + lane, 0], grad_hbm.at[slots(me), lane_columns(lane)],
+            local_sems.at[LINE + 1 + LANES + lane],
+        )
+
+    def gather(way, lane):
+        if way == 0:
+            lane_local(lane).wait()
+        lane_arrive(2 * way, lane)
+        at = LANES * way + lane
+        lane_pack[at] = lax.dot_general(
+            choose[way], lane_in[at], (((0,), (0,)), ((), ())),
             preferred_element_type=jnp.float32,
         ).astype(jnp.bfloat16)
-        cross(lane).start()
-
-    def spread(lane):
-        cross(lane).wait_recv()
+        cross(at).start()
+
+    def spread(way, lane):
+        at = LANES * way + lane
+        cross(at).wait_recv()
         for k in list(range(1, experts)) + [0]:
             rows_out = jnp.dot(
-                choose[1 - lane, slots(peer(k)), :], lane_got[lane],
+                choose[1 - way, slots(peer(k)), :], lane_got[at],
                 preferred_element_type=jnp.float32,
             ).astype(jnp.bfloat16)
-            if lane == 0:
+            if way == 0 and k == 0:
+                pre_theirs[lane_unit(lane), slots(me), :] = rows_out
+            else:
+                lane_out[at, k] = rows_out
                 if k == 0:
-                    pre_theirs[own, slots(me), :] = rows_out
+                    lane_home(lane).start()
                 else:
-                    lane_out[0, k - 1] = rows_out
-                    lane_copy(1, k).start()
-            else:
-                lane_out[1, k] = rows_out
-                if k == 0:
-                    lane_home.start()
-                else:
-                    lane_copy(3, k).start()
+                    lane_copy(2 * way + 1, lane, k).start()
 
     strip = 64
 
@@ -371,7 +378,7 @@
             activate_rows(0, i, pre_own, cut)
 
     def activate_theirs(i, cut):
-        if i < own:
+        if i < direct:
             pre_copy(i, cut).wait_recv()
         activate_rows(1, i, pre_theirs, cut)
 
@@ -385,44 +392,55 @@
             hidden[1, i, :, at], arrived[1, :, wide], (((0,), (0,)), ((), ())),
             preferred_element_type=jnp.float32,
         )
-        if i < own:
-            pass_on(i, True, cut, half)
-
-    def sum_copy(direction, stage, cut, half):
-        at, wide = within(cut), across(half)
-        return remote(
-            sums_out.at[direction, stage, at, wide], sums_in.at[direction, stage, at, wide],
-            sum_send.at[direction, stage, cut, half], sum_recv.at[direction, stage, cut, half],
-            {"dp": d + (1 - 2 * direction) * PAIR},
-        )
-
-    def pass_on(i, ends, cut, half):
+
+    def terms(i):
+        for cut in range(CUTS):
+            for half in range(HALVES):
+                term(i, cut, half)
+            if i < own:
+                begin(i, cut)
+
+    def pieces(stage):
+        return range(HALVES) if stage == 0 else (None,)
+
+    def sum_copy(direction, stage, cut, half, i=0):
+        at = within(cut)
+        wide = pl.ds(0, width) if half is None else across(half)
+        target = landed.at[direction] if stage == LINE - 2 else sums_in.at[direction, stage]
+        slot = (direction, stage, cut, half or 0)
+        return remote(
+            sums_out.at[i, at, wide], target.at[at, wide],
+            sum_send.at[slot], sum_recv.at[slot], {"dp": d + (1 - 2 * direction) * PAIR},
+        )
+
+    def toward(i, direction, ends):
         j = order(i)
-        at, wide = within(cut), across(half)
+        away = (j > z) if direction == 0 else (j < z)
+        first = (z == 0) if direction == 0 else (z == LINE - 1)
+        return away & first if ends else away & jnp.logical_not(first)
+
+    def begin(i, cut, half=None):
+        at = within(cut)
+        wide = pl.ds(0, width) if half is None else across(half)
         for direction in range(2):
-            distance = (j - z) if direction == 0 else (z - j)
-            first = (z == 0) if direction == 0 else (z == LINE - 1)
-            stage = jnp.clip(LINE - 1 - distance, 0, LINE - 2)
-            if ends:
-                @pl.when((distance > 0) & first)
-                def _():
-                    sums_out[direction, stage, at, wide] = partial[i, at, wide].astype(
-                        jnp.bfloat16
-                    )
-                    sum_copy(direction, stage, cut, half).start()
-            else:
-                @pl.when((distance > 0) & jnp.logical_not(first))
-                def _():
-                    last = jnp.clip(stage - 1, 0, LINE - 2)
-                    sum_copy(direction, last, cut, half).wait_recv()
-                    sums_out[direction, stage, at, wide] = (
-                        partial[i, at, wide]
-                        + sums_in[direction, last, at, wide].astype(jnp.float32)
-                    ).astype(jnp.bfloat16)
-                    sum_copy(direction, stage, cut, half).start()
-
-    def forward(i, chunk):
-        pass_on(i, False, *chunk)
+            @pl.when(toward(i, direction, True))
+            def _():
+                sums_out[i, at, wide] = partial[i, at, wide].astype(jnp.bfloat16)
+                sum_copy(direction, i, cut, half, i).start()
+
+    def forward(i, cut):
+        at = within(cut)
+        stage = min(i + 1, LINE - 2)
+        for direction in range(2):
+            @pl.when(toward(i, direction, False))
+            def _():
+                for half in pieces(stage - 1):
+                    sum_copy(direction, stage - 1, cut, half).wait_recv()
+                sums_out[i, at, :] = (
+                    partial[i, at, :]
+                    + sums_in[direction, stage - 1, at, :].astype(jnp.float32)
+                ).astype(jnp.bfloat16)
+                sum_copy(direction, stage, cut, None, i).start()
 
     def grad_copy(i):
         return remote(
@@ -458,15 +476,14 @@
 
         if rep == 0:
             grad_write(i).start()
-        elif i < own:
+        elif i < direct:
             grad_copy(i).start()
         else:
             for k in range(1, experts):
-                lane_copy(2, k).start()
-            lane_in[1, slots(me), :] = pre_theirs[own, slots(me), :]
+                lane_copy(2, own - i, k).start()
+            lane_in[LANES + own - i, slots(me), :] = pre_theirs[i, slots(me), :]
 
     route_load.wait()
-    token_load.wait()
     plan(0, own_route)
     dispatch(0, own_tokens, 0)
     activate_own(0)
@@ -480,115 +497,92 @@
     weight_arrive(0, 0)
     token_copy(1).wait_recv()
     dispatch(1, their_tokens, 1)
-    lane_local.start()
-    for k in range(1, experts):
-        lane_copy(0, k).start()
+    for lane in range(LANES):
+        lane_local(lane).start()
+        for k in range(1, experts):
+            lane_copy(0, lane, k).start()
     activate_own(own)
+    for rep in range(2):
+        tokens_arrive(rep, 0)
+    for cut in range(CUTS):
+        activate_theirs(0, cut)
+        term(0, cut, 0)
+        begin(0, cut, 0)
     weight_arrive(0, 1)
     for rep in range(2):
-        tokens_arrive(rep, 0)
-    activate_theirs(0, 0)
-    term(0, 0, 0)
-    weight_arrive(0, 2)
-    activate_theirs(0, 1)
-    term(0, 1, 0)
-    weight_arrive(0, 3)
-    for rep in range(2):
         tokens_arrive(rep, 1)
-    term(0, 0, 1)
-    term(0, 1, 1)
-    weight_own.wait()
+    for cut in range(CUTS):
+        term(0, cut, 1)
+        begin(0, cut, 1)
     differentiate(0, own)
     differentiate(0, own - 1)
-    lane_local.wait()
-    lane_arrive(0)
-    gather(0)
-    for cut in range(CUTS):
-        pre_copy(own - 1, cut).start()
+    gather(0, 0)
+    activate_theirs(1, 0)
     weight_arrive(1, 0)
-    forward(0, chunks[0])
-    activate_theirs(1, 0)
+    gather(0, 1)
+    activate_theirs(1, 1)
+    forward(0, 0)
+    terms(1)
+    spread(0, 0)
+    forward(0, 1)
     weight_arrive(1, 1)
-    forward(0, chunks[1])
-    activate_theirs(1, 1)
-    for chunk in chunks:
-        term(1, *chunk)
-    weight_arrive(1, 2)
-    forward(0, chunks[2])
-    spread(0)
-    weight_arrive(1, 3)
-    forward(0, chunks[3])
+    spread(0, 1)
     differentiate(1, 1)
     differentiate(0, 1)
-    lane_arrive(1)
+    lane_arrive(1, 0)
     for cut in range(CUTS):
         activate_theirs(own, cut)
     differentiate(1, own)
+    terms(own)
+    term_copy = pltpu.make_async_copy(
+        partial.at[own], term_out, local_sems.at[LINE + 1 + 2 * LANES]
+    )
+    term_copy.start()
+    lane_arrive(1, 1)
     for cut in range(CUTS):
-        activate_theirs(2, cut)
-    for chunk in chunks:
-        term(2, *chunk)
-    differentiate(1, 2)
-    forward(1, chunks[0])
-    forward(2, chunks[0])
-    for chunk in chunks:
-        term(own, *chunk)
-    lane_arrive(2)
-    gather(1)
-    for c in range(2):
-        weight_arrive(2, c)
-    forward(1, chunks[1])
-    forward(2, chunks[1])
-    forward(1, chunks[2])
-    forward(2, chunks[2])
-    for c in range(2, PARTS):
-        weight_arrive(2, c)
+        activate_theirs(own - 1, cut)
+    terms(own - 1)
+    differentiate(1, own - 1)
+    forward(1, 0)
+    forward(2, 0)
+    weight_arrive(2, 0)
+    gather(1, 0)
+    gather(1, 1)
+    forward(1, 1)
+    forward(2, 1)
+    weight_arrive(2, 1)
     differentiate(1, 0)
-    forward(1, chunks[3])
-    forward(2, chunks[3])
     differentiate(0, 0)
-
-    def result_copy(cut, half):
-        at, wide = within(cut), across(half)
-        return pltpu.make_async_copy(
-            partial.at[own, at, wide], dw_hbm.at[at, wide],
-            local_sems.at[LINE + 3 + cut * HALVES + half],
-        )
-
-    for n, (cut, half) in enumerate(chunks):
-        at, wide = within(cut), across(half)
-        for direction in range(2):
-            @pl.when(receives(direction, 0))
-            def _():
-                sum_copy(direction, LINE - 2, cut, half).wait_recv()
-                partial[own, at, wide] += sums_in[direction, LINE - 2, at, wide].astype(
-                    jnp.float32
-                )
-        partial[own, at, wide] = partial[own, at, wide] * factor
-        result_copy(cut, half).start()
-        if n == 1:
-            spread(1)
-
-    lane_arrive(3)
-    lane_home.wait()
+    for lane in range(LANES):
+        spread(1, lane)
+
+    for lane in range(LANES):
+        lane_arrive(3, lane)
+        lane_home(lane).wait()
     for i in range(LINE):
-        if i < own:
+        if i < direct:
             grad_arrive(i).wait_recv()
         grad_write(i).wait()
-    for cut, half in chunks:
-        result_copy(cut, half).wait()
+    term_copy.wait()
+    for direction in range(2):
+        @pl.when(receives(direction, 0))
+        def _():
+            for cut in range(CUTS):
+                sum_copy(direction, LINE - 2, cut, None).wait_recv()
     route_copy.wait_send()
     for half in range(HALVES):
         token_copy(half).wait_send()
-    for i in range(own):
+    for i in range(direct):
         for cut in range(CUTS):
             pre_copy(i, cut).wait_send()
         grad_copy(i).wait_send()
-    for lane in range(2):
+    for lane in range(LANES):
         cross(lane).wait_send()
+        cross(LANES + lane).wait_send()
     for k in range(1, experts):
         for leg in range(4):
-            lane_copy(leg, k).wait_send()
+            for lane in range(LANES):
+                lane_copy(leg, lane, k).wait_send()
         for rep in range(2):
             for half in range(HALVES):
                 dispatch_copy(rep, k, half).wait_send()
@@ -600,13 +594,40 @@
                     weight_copy(direction, hop, c).wait_send()
     for stage in range(LINE - 1):
         for direction in range(2):
-            toward = (z <= stage) if direction == 0 else (z >= LINE - 1 - stage)
+            sent = (z <= stage) if direction == 0 else (z >= LINE - 1 - stage)
             inside = (z < LINE - 1) if direction == 0 else (z > 0)
 
-            @pl.when(toward & inside)
+            @pl.when(sent & inside)
             def _():
-                for cut, half in chunks:
-                    sum_copy(direction, stage, cut, half).wait_send()
+                for cut in range(CUTS):
+                    for half in pieces(stage):
+                        sum_copy(direction, stage, cut, half).wait_send()
+
+
+def finish(factor, grad_ref, term_ref, landed_ref, grad_hbm, dw_hbm, summed, sems):
+    z = lax.div(lax.axis_index("dp"), PAIR)
+    rows, block = grad_ref.shape[0], term_ref.shape[0]
+    steps = 4
+
+    def grad_write(c):
+        at = pl.ds(c * (rows // steps), rows // steps)
+        return pltpu.make_async_copy(grad_ref.at[at], grad_hbm.at[at], sems.at[0, c])
+
+    def sum_write(c):
+        at = pl.ds(c * (block // steps), block // steps)
+        return pltpu.make_async_copy(summed.at[at], dw_hbm.at[at], sems.at[1, c])
+
+    for c in range(steps):
+        grad_write(c).start()
+    for c in range(steps):
+        at = pl.ds(c * (block // steps), block // steps)
+        up = jnp.where(z > 0, landed_ref[0, at, :].astype(jnp.float32), 0.0)
+        down = jnp.where(z < LINE - 1, landed_ref[1, at, :].astype(jnp.float32), 0.0)
+        summed[at, :] = (term_ref[at, :] + up + down) * factor
+        sum_write(c).start()
+    for c in range(steps):
+        grad_write(c).wait()
+        sum_write(c).wait()
 
 
 def fused(out_grad, expert_of, pre_act, down_weight):
@@ -621,14 +642,15 @@
     hbm = pl.BlockSpec(memory_space=pltpu.HBM)
     anywhere = pl.BlockSpec(memory_space=pl.ANY)
     dma = pltpu.SemaphoreType.DMA
-    pre_grad, summed = pl.pallas_call(
-        functools.partial(kernel, experts, capacity, factor),
+    placed = pl.pallas_call(
+        functools.partial(kernel, experts, capacity),
         out_shape=(
             pltpu.VMEM((rows, units), half),
             pltpu.VMEM((block, width), full),
+            pltpu.VMEM((2, block, width), half),
         ),
         in_specs=[hbm, hbm, hbm, hbm],
-        out_specs=(anywhere, anywhere),
+        out_specs=(anywhere, anywhere, anywhere),
         scratch_shapes=[
             pltpu.VMEM((count, width), half),
             pltpu.VMEM((1, count), jnp.int32),
@@ -639,25 +661,25 @@
             pltpu.VMEM((2, rows, width), half),
             pltpu.VMEM((LINE, rows, block), half),
             pltpu.VMEM((LINE, rows, block), half),
-            pltpu.VMEM((2, rows, block), half),
-            pltpu.VMEM((2, count, block), half),
-            pltpu.VMEM((2, count, block), half),
-            pltpu.VMEM((2, experts, capacity, block), half),
+            pltpu.VMEM((2 * LANES, rows, block), half),
+            pltpu.VMEM((2 * LANES, count, block), half),
+            pltpu.VMEM((2 * LANES, count, block), half),
+            pltpu.VMEM((2 * LANES, experts, capacity, block), half),
             pltpu.VMEM((LINE, block, width), half),
             pltpu.VMEM((2, LINE, rows, block), half),
             pltpu.VMEM((2, LINE, rows, block), full),
             pltpu.VMEM((LINE, block, width), full),
-            pltpu.VMEM((2, LINE - 1, block, width), half),
-            pltpu.VMEM((2, LINE - 1, block, width), half),
+            pltpu.VMEM((LINE - 1, block, width), half),
+            pltpu.VMEM((2, LINE - 2, block, width), half),
             dma((2,)),
             dma((2, HALVES + 1)),
             dma((2, experts - 1, HALVES)),
             dma((2, experts - 1, HALVES)),
-            dma((LINE + 3 + CUTS * HALVES,)),
-            dma((2, LINE - 1, CUTS)),
-            dma((4, experts - 1)),
-            dma((4, experts - 1)),
-            dma((2, 2)),
+            dma((LINE + 2 + 2 * LANES,)),
+            dma((2, LINE - LANES, CUTS)),
+            dma((4, LANES, experts - 1)),
+            dma((4, LANES, experts - 1)),
+            dma((2, 2 * LANES)),
             dma((2, LINE - 1, PARTS)),
             dma((2, LINE - 1, PARTS)),
             dma((2, LINE - 1, CUTS, HALVES)),
@@ -671,6 +693,18 @@
         pltpu.with_memory_space_constraint(array, pltpu.HBM)
         for array in (out_grad, expert_of.reshape(1, count), pre_act, down_weight[0])
     ))
+    vmem = pl.BlockSpec(memory_space=pltpu.VMEM)
+    pre_grad, summed = pl.pallas_call(
+        functools.partial(finish, factor),
+        out_shape=(
+            jax.ShapeDtypeStruct((rows, units), half),
+            jax.ShapeDtypeStruct((block, width), full),
+        ),
+        in_specs=[vmem, vmem, vmem],
+        out_specs=(hbm, hbm),
+        scratch_shapes=[pltpu.VMEM((block, width), full), dma((2, 4))],
+        compiler_params=pltpu.CompilerParams(vmem_limit_bytes=16 * 1024 * 1024),
+    )(*placed)
     return pre_grad, summed.reshape(1, block, width)
 
 

time: 102 us -> 101 us (level)
  local copies, waits for them, and re-layouts: 3.33 us -> 0 us
  Pallas kernels: 97.8 us -> 100 us
    unnamed x2 -> x0, local copies, waits for them, and re-layouts: 3.33 us -> none
    pallas_call x1 -> x2, Pallas kernels: 97.8 us -> 100 us  [the longest x1 97.3 us: fused(): pl.pallas_call(functools.partial(kernel, experts, capacity), out_shape=(p...]
where the time goes in v3:
time: 101 us
  Pallas kernels  100 us (99%)
    pallas_call x1, Pallas kernels, fused(): pl.pallas_call(functools.partial(kernel, experts, capacity), out_shape=(p...  97.3 us
    pallas_call x1, Pallas kernels, fused(): pl.pallas_call(functools.partial(finish, factor), out_shape=(jax.ShapeDty...  2.72 us

profile of v3, /device:TPU:0, one launch (start us, length us, event | category | flops | bytes accessed | tf_op | source)
XLA Modules:
  0.0 100.8 jit_solution(15549726948338747487)
XLA Ops:
  0.6 97.3 %shard_map.59 = (bf16[512,4096]{1,0:T(8,128)(2,1)S(1)}, f32[512,1024]{1,0:T(8,128)S(1)}, bf16[2,512,1024]{2,1,0:T(8,128)(2,1)S(1)}) custom-call(bf16[256,1024]{1,0:T(8,128)(2,1)} %tokens_hbm.1, s32[1,256]{1,0:T(1,128)} %bitcast.4, bf16[512,4096]{1,0:T(8,128)(2,1)} %pre_hbm.1, bf16[512,1024]{1,0:T(8,128)(2,1)} %bitcast.3), custom_call_target="tpu_custom_call" | custom-call | tf_op jit(solution)/shard_map/pallas_call | solution.py:645
  97.9 2.7 %shard_map.60 = (bf16[512,4096]{1,0:T(8,128)(2,1)}, f32[512,1024]{1,0:T(8,128)}) custom-call(bf16[512,4096]{1,0:T(8,128)(2,1)S(1)} %get-tuple-element.7.grad_ref, f32[512,1024]{1,0:T(8,128)S(1)} %get-tuple-element.8.term_ref, bf16[2,512,1024]{2,1,0:T(8,128)(2,1)S(1)} %get-tuple-element.9.landed_ref), custom_call_target="tpu_custom_call" | custom-call | tf_op jit(solution)/shard_map/pallas_call | solution.py:697

commit v4 on v3

--- a/solution.py
+++ b/solution.py
@@ -146,14 +146,14 @@
         )
 
     route_copy = remote(
-        route_hbm, their_route, token_sems.at[0, HALVES], token_sems.at[1, HALVES],
+        route_hbm, their_route, token_sems.at[0], token_sems.at[1],
         {"dp": partner},
     )
 
     def token_copy(half):
         return remote(
             own_tokens.at[:, across(half)], their_tokens.at[:, across(half)],
-            token_sems.at[0, half], token_sems.at[1, half], {"dp": partner},
+            token_sems.at[2], token_sems.at[3 + half], {"dp": partner},
         )
 
     def pre_copy(i, cut):
@@ -161,13 +161,13 @@
         return remote(
             pre_hbm.at[:, pl.ds(pl.multiple_of(start, piece), piece)],
             pre_theirs.at[i, :, within(cut)],
-            pre_sems.at[0, i, cut], pre_sems.at[1, i, cut], {"dp": partner},
+            pre_sems.at[0], pre_sems.at[1 + i * CUTS + cut], {"dp": partner},
         )
 
     def cross(lane):
         return remote(
             lane_pack.at[lane], lane_got.at[lane],
-            cross_sems.at[0, lane], cross_sems.at[1, lane], {"dp": partner},
+            cross_sems.at[0], cross_sems.at[1 + lane], {"dp": partner},
         )
 
     def part(c):
@@ -177,8 +177,8 @@
         step = 1 - 2 * direction
         shard = jnp.clip(z - step * hop, 0, LINE - 1)
         return remote(
-            weights.at[shard, part(c)], weights.at[shard, part(c)], weight_send.at[direction, hop, c],
-            weight_recv.at[direction, hop, c], {"dp": d + step * PAIR},
+            weights.at[shard, part(c)], weights.at[shard, part(c)], weight_send.at[direction],
+            weight_recv.at[shard, c], {"dp": d + step * PAIR},
         )
 
     def sends(direction, hop):
@@ -203,8 +203,7 @@
                 shard = jnp.clip(z - step * (hop + 1), 0, LINE - 1)
                 remote(
                     weight_hbm.at[part(c)], weights.at[shard, part(c)],
-                    weight_send.at[direction, hop, c],
-                    weight_recv.at[direction, hop, c], {"dp": partner},
+                    weight_send.at[direction], weight_recv.at[shard, c], {"dp": partner},
                 ).wait_recv()
 
         if hop < LINE - 2:
@@ -252,8 +251,8 @@
         return remote(
             outgoing.at[rep, k - 1, :, across(half)],
             arrived.at[rep, slots(me), across(half)],
-            dispatch_send.at[rep, k - 1, half],
-            dispatch_recv.at[rep, k - 1, half],
+            dispatch_send.at[0],
+            dispatch_recv.at[half],
             {"expert": peer(k)},
         )
 
@@ -269,15 +268,13 @@
                 outgoing[rep, k - 1, :, across(half)] = rows_out
                 dispatch_copy(rep, k, half).start()
 
-    def tokens_arrive(rep, half):
-        for k in range(1, experts):
-            remote(
-                outgoing.at[rep, k - 1, :, across(half)],
-                arrived.at[rep, slots(from_peer(k)), across(half)],
-                dispatch_send.at[rep, k - 1, half],
-                dispatch_recv.at[rep, k - 1, half],
-                {"expert": peer(k)},
-            ).wait_recv()
+    peers = pl.ds(0, (experts - 1) * capacity)
+
+    def tokens_arrive(half):
+        came = arrived.at[:, peers, across(half)]
+        remote(
+            came, came, dispatch_send.at[0], dispatch_recv.at[half], {"expert": peer(1)}
+        ).wait_recv()
 
     def lane_unit(lane):
         return own - lane
@@ -302,17 +299,15 @@
         else:
             src = lane_out.at[lane + LANES * (leg // 2), k]
         return remote(
-            src, lane_target(leg, lane, me), lane_send.at[leg, lane, k - 1],
-            lane_recv.at[leg, lane, k - 1], {"expert": peer(k)},
+            src, lane_target(leg, lane, me), lane_send.at[leg // 2], lane_recv.at[leg, lane],
+            {"expert": peer(k)},
         )
 
     def lane_arrive(leg, lane):
-        for k in range(1, experts):
-            remote(
-                lane_out.at[lane, k], lane_target(leg, lane, from_peer(k)),
-                lane_send.at[leg, lane, k - 1], lane_recv.at[leg, lane, k - 1],
-                {"expert": peer(k)},
-            ).wait_recv()
+        came = lane_in.at[lane, peers]
+        remote(
+            came, came, lane_send.at[0], lane_recv.at[leg, lane], {"expert": peer(1)}
+        ).wait_recv()
 
     def lane_local(lane):
         return pltpu.make_async_copy(
@@ -323,7 +318,7 @@
     def lane_home(lane):
         return pltpu.make_async_copy(
             lane_out.at[LANES + lane, 0], grad_hbm.at[slots(me), lane_columns(lane)],
-            local_sems.at[LINE + 1 + LANES + lane],
+            local_sems.at[LINE + 1 + LANES],
         )
 
     def gather(way, lane):
@@ -407,10 +402,13 @@
         at = within(cut)
         wide = pl.ds(0, width) if half is None else across(half)
         target = landed.at[direction] if stage == LINE - 2 else sums_in.at[direction, stage]
-        slot = (direction, stage, cut, half or 0)
+        if stage == 0:
+            slot = cut * HALVES + half
+        else:
+            slot = CUTS * HALVES + (cut if stage == 1 else CUTS)
         return remote(
-            sums_out.at[i, at, wide], target.at[at, wide],
-            sum_send.at[slot], sum_recv.at[slot], {"dp": d + (1 - 2 * direction) * PAIR},
+            sums_out.at[i, at, wide], target.at[at, wide], sum_send.at[direction],
+            sum_recv.at[direction, slot], {"dp": d + (1 - 2 * direction) * PAIR},
         )
 
     def toward(i, direction, ends):
@@ -445,18 +443,12 @@
     def grad_copy(i):
         return remote(
             pre_theirs.at[i], grad_hbm.at[:, columns(order(i), x)],
-            grad_sems.at[0, i], grad_sems.at[1, i], {"dp": partner},
-        )
-
-    def grad_arrive(i):
-        return remote(
-            pre_theirs.at[i], grad_hbm.at[:, columns(order(i), 1 - x)],
-            grad_sems.at[0, i], grad_sems.at[1, i], {"dp": partner},
+            grad_sems.at[0], grad_sems.at[1], {"dp": partner},
         )
 
     def grad_write(i):
         return pltpu.make_async_copy(
-            pre_own.at[i], grad_hbm.at[:, columns(order(i), x)], grad_sems.at[2, i]
+            pre_own.at[i], grad_hbm.at[:, columns(order(i), x)], grad_sems.at[2]
         )
 
     tile = 256
@@ -502,15 +494,13 @@
         for k in range(1, experts):
             lane_copy(0, lane, k).start()
     activate_own(own)
-    for rep in range(2):
-        tokens_arrive(rep, 0)
+    tokens_arrive(0)
     for cut in range(CUTS):
         activate_theirs(0, cut)
         term(0, cut, 0)
         begin(0, cut, 0)
     weight_arrive(0, 1)
-    for rep in range(2):
-        tokens_arrive(rep, 1)
+    tokens_arrive(1)
     for cut in range(CUTS):
         term(0, cut, 1)
         begin(0, cut, 1)
@@ -535,7 +525,7 @@
     differentiate(1, own)
     terms(own)
     term_copy = pltpu.make_async_copy(
-        partial.at[own], term_out, local_sems.at[LINE + 1 + 2 * LANES]
+        partial.at[own], term_out, local_sems.at[LINE + 2 + LANES]
     )
     term_copy.start()
     lane_arrive(1, 1)
@@ -558,75 +548,77 @@
 
     for lane in range(LANES):
         lane_arrive(3, lane)
-        lane_home(lane).wait()
-    for i in range(LINE):
-        if i < direct:
-            grad_arrive(i).wait_recv()
-        grad_write(i).wait()
+    home = lane_out.at[pl.ds(LANES, LANES), 0]
+    pltpu.make_async_copy(home, home, local_sems.at[LINE + 1 + LANES]).wait()
+    units = pre_theirs.at[pl.ds(0, direct)]
+    returned = remote(units, units, grad_sems.at[0], grad_sems.at[1], {"dp": partner})
+    returned.wait_recv()
+    pltpu.make_async_copy(pre_own, pre_own, grad_sems.at[2]).wait()
     term_copy.wait()
     for direction in range(2):
         @pl.when(receives(direction, 0))
         def _():
-            for cut in range(CUTS):
-                sum_copy(direction, LINE - 2, cut, None).wait_recv()
+            whole = landed.at[direction]
+            remote(
+                whole, whole, sum_send.at[direction],
+                sum_recv.at[direction, CUTS * HALVES + CUTS], {"dp": partner},
+            ).wait_recv()
+
     route_copy.wait_send()
-    for half in range(HALVES):
-        token_copy(half).wait_send()
-    for i in range(direct):
-        for cut in range(CUTS):
-            pre_copy(i, cut).wait_send()
-        grad_copy(i).wait_send()
-    for lane in range(LANES):
-        cross(lane).wait_send()
-        cross(LANES + lane).wait_send()
-    for k in range(1, experts):
-        for leg in range(4):
-            for lane in range(LANES):
-                lane_copy(leg, lane, k).wait_send()
-        for rep in range(2):
-            for half in range(HALVES):
-                dispatch_copy(rep, k, half).wait_send()
-    for hop in range(LINE - 1):
+    remote(
+        own_tokens, their_tokens, token_sems.at[2], token_sems.at[3], {"dp": partner}
+    ).wait_send()
+    remote(units, units, pre_sems.at[0], pre_sems.at[1], {"dp": partner}).wait_send()
+    returned.wait_send()
+    remote(
+        lane_pack, lane_got, cross_sems.at[0], cross_sems.at[1], {"dp": partner}
+    ).wait_send()
+    remote(
+        outgoing, outgoing, dispatch_send.at[0], dispatch_recv.at[0], {"expert": peer(1)}
+    ).wait_send()
+    lanes_sent = lane_in.at[:, peers]
+    for way in range(2):
+        remote(
+            lanes_sent, lanes_sent, lane_send.at[way], lane_recv.at[0, 0], {"expert": peer(1)}
+        ).wait_send()
+    for n in range(1, LINE):
         for direction in range(2):
-            @pl.when(sends(direction, hop))
+            @pl.when(z == (n - 1 if direction == 0 else LINE - n))
             def _():
-                for c in range(PARTS):
-                    weight_copy(direction, hop, c).wait_send()
-    for stage in range(LINE - 1):
-        for direction in range(2):
-            sent = (z <= stage) if direction == 0 else (z >= LINE - 1 - stage)
-            inside = (z < LINE - 1) if direction == 0 else (z > 0)
-
-            @pl.when(sent & inside)
+                shards = weights.at[pl.ds(0, n)]
+                remote(
+                    shards, shards, weight_send.at[direction], weight_recv.at[0, 0],
+                    {"dp": partner},
+                ).wait_send()
+
+            @pl.when(z == (LINE - 1 - n if direction == 0 else n))
             def _():
-                for cut in range(CUTS):
-                    for half in pieces(stage):
-                        sum_copy(direction, stage, cut, half).wait_send()
+                sent = sums_out.at[pl.ds(0, n)]
+                remote(
+                    sent, sent, sum_send.at[direction], sum_recv.at[direction, 0],
+                    {"dp": partner},
+                ).wait_send()
 
 
 def finish(factor, grad_ref, term_ref, landed_ref, grad_hbm, dw_hbm, summed, sems):
     z = lax.div(lax.axis_index("dp"), PAIR)
-    rows, block = grad_ref.shape[0], term_ref.shape[0]
-    steps = 4
-
-    def grad_write(c):
-        at = pl.ds(c * (rows // steps), rows // steps)
-        return pltpu.make_async_copy(grad_ref.at[at], grad_hbm.at[at], sems.at[0, c])
+    block = term_ref.shape[0]
+    steps = 2
 
     def sum_write(c):
         at = pl.ds(c * (block // steps), block // steps)
-        return pltpu.make_async_copy(summed.at[at], dw_hbm.at[at], sems.at[1, c])
-
-    for c in range(steps):
-        grad_write(c).start()
+        return pltpu.make_async_copy(summed.at[at], dw_hbm.at[at], sems.at[1 + c])
+
+    grad_write = pltpu.make_async_copy(grad_ref, grad_hbm, sems.at[0])
+    grad_write.start()
     for c in range(steps):
         at = pl.ds(c * (block // steps), block // steps)
         up = jnp.where(z > 0, landed_ref[0, at, :].astype(jnp.float32), 0.0)
         down = jnp.where(z < LINE - 1, landed_ref[1, at, :].astype(jnp.float32), 0.0)
         summed[at, :] = (term_ref[at, :] + up + down) * factor
         sum_write(c).start()
+    grad_write.wait()
     for c in range(steps):
-        grad_write(c).wait()
         sum_write(c).wait()
 
 
@@ -672,19 +664,19 @@
             pltpu.VMEM((LINE - 1, block, width), half),
             pltpu.VMEM((2, LINE - 2, block, width), half),
             dma((2,)),
-            dma((2, HALVES + 1)),
-            dma((2, experts - 1, HALVES)),
-            dma((2, experts - 1, HALVES)),
-            dma((LINE + 2 + 2 * LANES,)),
-            dma((2, LINE - LANES, CUTS)),
-            dma((4, LANES, experts - 1)),
-            dma((4, LANES, experts - 1)),
-            dma((2, 2 * LANES)),
-            dma((2, LINE - 1, PARTS)),
-            dma((2, LINE - 1, PARTS)),
-            dma((2, LINE - 1, CUTS, HALVES)),
-            dma((2, LINE - 1, CUTS, HALVES)),
-            dma((3, LINE)),
+            dma((3 + HALVES,)),
+            dma((1,)),
+            dma((HALVES,)),
+            dma((LINE + 3 + LANES,)),
+            dma((1 + (LINE - LANES) * CUTS,)),
+            dma((2,)),
+            dma((4, LANES)),
+            dma((1 + 2 * LANES,)),
+            dma((2,)),
+            dma((LINE, PARTS)),
+            dma((2,)),
+            dma((2, CUTS * HALVES + CUTS + 1)),
+            dma((3,)),
         ],
         compiler_params=pltpu.CompilerParams(
             collective_id=0, has_side_effects=True, vmem_limit_bytes=51 * 1024 * 1024
@@ -702,7 +694,7 @@
         ),
         in_specs=[vmem, vmem, vmem],
         out_specs=(hbm, hbm),
-        scratch_shapes=[pltpu.VMEM((block, width), full), dma((2, 4))],
+        scratch_shapes=[pltpu.VMEM((block, width), full), dma((3,))],
         compiler_params=pltpu.CompilerParams(vmem_limit_bytes=16 * 1024 * 1024),
     )(*placed)
     return pre_grad, summed.reshape(1, block, width)

time: 101 us -> 99.8 us (0.988)
  Pallas kernels: 100 us -> 98.8 us
    pallas_call x1, Pallas kernels: 97.3 us -> 96.1 us  [fused(): pl.pallas_call(functools.partial(kernel, experts, capacity), out_shape=(p...]
where the time goes in v4:
time: 99.8 us; the launch traced here: 99.6 us
  Pallas kernels  98.8 us (99%)
    pallas_call x1, Pallas kernels, fused(): pl.pallas_call(functools.partial(kernel, experts, capacity), out_shape=(p...  96.1 us
    pallas_call x1, Pallas kernels, fused(): pl.pallas_call(functools.partial(finish, factor), out_shape=(jax.ShapeDty...  2.69 us

profile of v4, /device:TPU:0, one launch (start us, length us, event | category | flops | bytes accessed | tf_op | source)
XLA Modules:
  0.0 99.6 jit_solution(11766701576312421050)
XLA Ops:
  0.6 96.1 %shard_map.59 = (bf16[512,4096]{1,0:T(8,128)(2,1)S(1)}, f32[512,1024]{1,0:T(8,128)S(1)}, bf16[2,512,1024]{2,1,0:T(8,128)(2,1)S(1)}) custom-call(bf16[256,1024]{1,0:T(8,128)(2,1)} %tokens_hbm.1, s32[1,256]{1,0:T(1,128)} %bitcast.4, bf16[512,4096]{1,0:T(8,128)(2,1)} %pre_hbm.1, bf16[512,1024]{1,0:T(8,128)(2,1)} %bitcast.3), custom_call_target="tpu_custom_call" | custom-call | tf_op jit(solution)/shard_map/pallas_call | solution.py:637
  96.8 2.7 %shard_map.60 = (bf16[512,4096]{1,0:T(8,128)(2,1)}, f32[512,1024]{1,0:T(8,128)}) custom-call(bf16[512,4096]{1,0:T(8,128)(2,1)S(1)} %get-tuple-element.7.grad_ref, f32[512,1024]{1,0:T(8,128)S(1)} %get-tuple-element.8.term_ref, bf16[2,512,1024]{2,1,0:T(8,128)(2,1)S(1)} %get-tuple-element.9.landed_ref), custom_call_target="tpu_custom_call" | custom-call | tf_op jit(solution)/shard_map/pallas_call | solution.py:689

commit v5 on v4

--- a/solution.py
+++ b/solution.py
@@ -116,7 +116,7 @@
 
     route_load = pltpu.make_async_copy(route_hbm, own_route, input_sems.at[0])
     token_load = pltpu.make_async_copy(tokens_hbm, own_tokens, input_sems.at[1])
-    weight_own = pltpu.make_async_copy(weight_hbm, weights.at[z], local_sems.at[LINE])
+    weight_own = pltpu.make_async_copy(weight_hbm, weights.at[z], local_sems.at[1])
     weight_own.start()
     route_load.start()
     token_load.start()
@@ -161,7 +161,7 @@
         return remote(
             pre_hbm.at[:, pl.ds(pl.multiple_of(start, piece), piece)],
             pre_theirs.at[i, :, within(cut)],
-            pre_sems.at[0], pre_sems.at[1 + i * CUTS + cut], {"dp": partner},
+            grad_sems.at[0], pre_sems.at[i * CUTS + cut], {"dp": partner},
         )
 
     def cross(lane):
@@ -222,7 +222,7 @@
 
     def own_copy(i):
         return pltpu.make_async_copy(
-            pre_hbm.at[:, columns(order(i), x)], pre_own.at[i], local_sems.at[i]
+            pre_hbm.at[:, columns(order(i), x)], pre_own.at[i], local_sems.at[0]
         )
 
     for i in range(LINE):
@@ -312,13 +312,13 @@
     def lane_local(lane):
         return pltpu.make_async_copy(
             pre_hbm.at[slots(me), lane_columns(lane)], lane_in.at[lane, slots(me)],
-            local_sems.at[LINE + 1 + lane],
+            local_sems.at[4 + lane],
         )
 
     def lane_home(lane):
         return pltpu.make_async_copy(
             lane_out.at[LANES + lane, 0], grad_hbm.at[slots(me), lane_columns(lane)],
-            local_sems.at[LINE + 1 + LANES],
+            local_sems.at[2],
         )
 
     def gather(way, lane):
@@ -368,7 +368,6 @@
                 hidden[rep, i, at, at_columns] = (v * gate).astype(jnp.bfloat16)
 
     def activate_own(i):
-        own_copy(i).wait()
         for cut in range(CUTS):
             activate_rows(0, i, pre_own, cut)
 
@@ -395,17 +394,11 @@
             if i < own:
                 begin(i, cut)
 
-    def pieces(stage):
-        return range(HALVES) if stage == 0 else (None,)
-
     def sum_copy(direction, stage, cut, half, i=0):
         at = within(cut)
         wide = pl.ds(0, width) if half is None else across(half)
         target = landed.at[direction] if stage == LINE - 2 else sums_in.at[direction, stage]
-        if stage == 0:
-            slot = cut * HALVES + half
-        else:
-            slot = CUTS * HALVES + (cut if stage == 1 else CUTS)
+        slot = min(stage * CUTS + cut, 2 * CUTS)
         return remote(
             sums_out.at[i, at, wide], target.at[at, wide], sum_send.at[direction],
             sum_recv.at[direction, slot], {"dp": d + (1 - 2 * direction) * PAIR},
@@ -432,8 +425,11 @@
         for direction in range(2):
             @pl.when(toward(i, direction, False))
             def _():
-                for half in pieces(stage - 1):
-                    sum_copy(direction, stage - 1, cut, half).wait_recv()
+                came = sums_in.at[direction, stage - 1, at]
+                remote(
+                    came, came, sum_send.at[direction],
+                    sum_recv.at[direction, (stage - 1) * CUTS + cut], {"dp": partner},
+                ).wait_recv()
                 sums_out[i, at, :] = (
                     partial[i, at, :]
                     + sums_in[direction, stage - 1, at, :].astype(jnp.float32)
@@ -478,6 +474,7 @@
     route_load.wait()
     plan(0, own_route)
     dispatch(0, own_tokens, 0)
+    pltpu.make_async_copy(pre_own, pre_own, local_sems.at[0]).wait()
     activate_own(0)
     activate_own(1)
     route_copy.wait_recv()
@@ -525,7 +522,7 @@
     differentiate(1, own)
     terms(own)
     term_copy = pltpu.make_async_copy(
-        partial.at[own], term_out, local_sems.at[LINE + 2 + LANES]
+        partial.at[own], term_out, local_sems.at[3]
     )
     term_copy.start()
     lane_arrive(1, 1)
@@ -549,7 +546,7 @@
     for lane in range(LANES):
         lane_arrive(3, lane)
     home = lane_out.at[pl.ds(LANES, LANES), 0]
-    pltpu.make_async_copy(home, home, local_sems.at[LINE + 1 + LANES]).wait()
+    pltpu.make_async_copy(home, home, local_sems.at[2]).wait()
     units = pre_theirs.at[pl.ds(0, direct)]
     returned = remote(units, units, grad_sems.at[0], grad_sems.at[1], {"dp": partner})
     returned.wait_recv()
@@ -561,15 +558,17 @@
             whole = landed.at[direction]
             remote(
                 whole, whole, sum_send.at[direction],
-                sum_recv.at[direction, CUTS * HALVES + CUTS], {"dp": partner},
+                sum_recv.at[direction, 2 * CUTS], {"dp": partner},
             ).wait_recv()
 
     route_copy.wait_send()
     remote(
         own_tokens, their_tokens, token_sems.at[2], token_sems.at[3], {"dp": partner}
     ).wait_send()
-    remote(units, units, pre_sems.at[0], pre_sems.at[1], {"dp": partner}).wait_send()
-    returned.wait_send()
+    crossed = hidden.at[:, pl.ds(0, direct)]
+    remote(
+        crossed, crossed, grad_sems.at[0], grad_sems.at[1], {"dp": partner}
+    ).wait_send()
     remote(
         lane_pack, lane_got, cross_sems.at[0], cross_sems.at[1], {"dp": partner}
     ).wait_send()
@@ -667,15 +666,15 @@
             dma((3 + HALVES,)),
             dma((1,)),
             dma((HALVES,)),
-            dma((LINE + 3 + LANES,)),
-            dma((1 + (LINE - LANES) * CUTS,)),
+            dma((4 + LANES,)),
+            dma(((LINE - LANES) * CUTS,)),
             dma((2,)),
             dma((4, LANES)),
             dma((1 + 2 * LANES,)),
             dma((2,)),
             dma((LINE, PARTS)),
             dma((2,)),
-            dma((2, CUTS * HALVES + CUTS + 1)),
+            dma((2, 2 * CUTS + 1)),
             dma((3,)),
         ],
         compiler_params=pltpu.CompilerParams(

time: 99.8 us -> 99.7 us (level)
  no operation moved by 1% of the time
where the time goes in v5:
time: 99.7 us; the launch traced here: 99.5 us
  Pallas kernels  98.7 us (99%)
    pallas_call x1, Pallas kernels, fused(): pl.pallas_call(functools.partial(kernel, experts, capacity), out_shape=(p...  96 us
    pallas_call x1, Pallas kernels, fused(): pl.pallas_call(functools.partial(finish, factor), out_shape=(jax.ShapeDty...  2.69 us

profile of v5, /device:TPU:0, one launch (start us, length us, event | category | flops | bytes accessed | tf_op | source)
XLA Modules:
  0.0 99.5 jit_solution(9076731750219700571)
XLA Ops:
  0.6 96.0 %shard_map.59 = (bf16[512,4096]{1,0:T(8,128)(2,1)S(1)}, f32[512,1024]{1,0:T(8,128)S(1)}, bf16[2,512,1024]{2,1,0:T(8,128)(2,1)S(1)}) custom-call(bf16[256,1024]{1,0:T(8,128)(2,1)} %tokens_hbm.1, s32[1,256]{1,0:T(1,128)} %bitcast.4, bf16[512,4096]{1,0:T(8,128)(2,1)} %pre_hbm.1, bf16[512,1024]{1,0:T(8,128)(2,1)} %bitcast.3), custom_call_target="tpu_custom_call" | custom-call | tf_op jit(solution)/shard_map/pallas_call | solution.py:636
  96.7 2.7 %shard_map.60 = (bf16[512,4096]{1,0:T(8,128)(2,1)}, f32[512,1024]{1,0:T(8,128)}) custom-call(bf16[512,4096]{1,0:T(8,128)(2,1)S(1)} %get-tuple-element.7.grad_ref, f32[512,1024]{1,0:T(8,128)S(1)} %get-tuple-element.8.term_ref, bf16[2,512,1024]{2,1,0:T(8,128)(2,1)S(1)} %get-tuple-element.9.landed_ref), custom_call_target="tpu_custom_call" | custom-call | tf_op jit(solution)/shard_map/pallas_call | solution.py:688
